TPU v7x, 128 devices: a whole 4x4x4 slice. The times are simulated.
128 devices in a mesh: freq: 64 (over x, y, z_hi, core), depth: 2 (over z_lo).
Axes of the slice: x: 4, y: 4, z: 4 (z_hi: 2, z_lo: 2; z = z_hi * 2 + z_lo), core: 2. Of those that a mesh axis runs over, the one named last changes fastest.
Arguments:
- pressure_field: bfloat16 [8192, 16384], P('depth', 'freq'), may hold values from -6 to 6
- block_main: bfloat16 [8192, 3, 2, 128], P('depth'), may hold values from -0.15625 to 0.15625
- block_coupled: bfloat16 [8192, 3, 2, 128], P('depth'), may hold values from -0.15625 to 0.15625
- coupling: float32 [16384], P('freq'), may hold values from -3 to 3
- frequencies: float32 [8192], replicated, may hold values from 1 to 1024
- receivers: int32 [512], replicated, may hold values from 0 to 8191
- floors: int32 [4], replicated, may hold values from 2048 to 8191
Outputs:
- series: float32 [512, 2048], P('depth', 'freq')
Inputs may be any that keep to these rules, and one draw needn't show every extreme that they name: `receivers`: any depth cells, repeats possible.
All inputs are finite; a program needn't handle non-finite values.
Results may differ from a plain program's by a relative error of at most 0.0061.
Values may be sent and summed in bfloat16 or wider, within the bound.
A program may use at most 256 MiB of HBM per device.

v0:
```python
import math

import jax
import jax.numpy as jnp
from jax import lax
from jax.sharding import PartitionSpec as P

NT = 2048
STEPS = 4


def padded_2(cells, sides, width):
    for axis, dim in sides:
        count = lax.axis_size(axis)
        ends = count - 1
        head = lax.slice_in_dim(cells, 0, width, axis=dim)
        tail = lax.slice_in_dim(cells, cells.shape[dim] - width, cells.shape[dim], axis=dim)
        cells = jnp.concatenate(
            [
                lax.ppermute(tail, axis, [(i, (i + 1) % count) for i in range(ends)]),
                cells,
                lax.ppermute(head, axis, [((i + 1) % count, i) for i in range(ends)]),
            ],
            axis=dim,
        )
    return cells


def in_blocks(x, dim, size):
    before, after = (x.shape[:dim], x.shape[dim + 1 :])
    return jnp.moveaxis(x.reshape(*before, size, -1, *after), dim, 0)


def summed_on_arrival(x, axis, dim):
    parts = in_blocks(x, dim, lax.axis_size(axis))
    arrived = lax.all_to_all(parts, axis, split_axis=0, concat_axis=0, tiled=True)
    return arrived.astype(jnp.float32).sum(axis=0)


def summed_on_arrival_2(x, axis, dim):
    parts = in_blocks(x, dim, lax.axis_size(axis))
    arrived = lax.all_to_all(parts, axis, split_axis=0, concat_axis=0, tiled=True)
    return arrived.sum(axis=0)


def times_unit(values):
    column = lax.broadcasted_iota(jnp.int32, values.shape, 1)
    upper = jnp.roll(values, -1, axis=1)
    lower = jnp.roll(values, 1, axis=1)
    return jnp.where(column % 2 == 0, -upper, lower)


def order_blocks(blocks, block_count, block_size):
    shaped = blocks.reshape(block_count, block_size, 3, 2, block_size)
    return shaped.transpose(0, 2, 3, 1, 4).reshape(block_count, 3, 2 * block_size, block_size)


def apply_blocks(ordered, padded, block_count, block_size):
    width = padded.shape[1]
    stacked = padded.reshape(block_count + 2, block_size, width)
    product = jnp.zeros((block_count, 2 * block_size, width), jnp.float32)
    for offset in range(3):
        product = product + jnp.einsum(
            "bij,bjc->bic",
            ordered[:, offset],
            stacked[offset : offset + block_count],
            preferred_element_type=jnp.float32,
        )
    real_part = product[:, :block_size].reshape(block_count * block_size, width)
    imag_part = product[:, block_size:].reshape(block_count * block_size, width)
    return real_part + times_unit(imag_part)


def make_basis(freq_values, sample_times):
    phase = jnp.mod(freq_values[:, None] * sample_times[None, :], jnp.float32(NT)) / jnp.float32(NT)
    angle = 2.0 * math.pi * phase
    stacked = jnp.stack([jnp.cos(angle), -jnp.sin(angle)], axis=1)
    return stacked.reshape(2 * freq_values.shape[0], sample_times.shape[0]).astype(jnp.bfloat16)


def local(pressure_field, block_main, block_coupled, coupling, frequencies, receivers, floors):
    rows_here = pressure_field.shape[0]
    block_size = block_main.shape[3]
    block_count = rows_here // block_size
    main_blocks = order_blocks(block_main, block_count, block_size)
    side_blocks = order_blocks(block_coupled, block_count, block_size)
    width = pressure_field.shape[1]
    column = jnp.arange(width, dtype=jnp.int32)
    even_weight = jnp.take(coupling, column - column % 2)
    odd_weight = jnp.take(coupling, column - column % 2 + 1)
    first_row = lax.axis_index("depth") * rows_here
    depth_index = first_row + jnp.arange(rows_here, dtype=jnp.int32)
    columns = pressure_field
    for step in range(STEPS):
        padded = padded_2(columns, (("depth", 0),), block_size)
        coupled = apply_blocks(side_blocks, padded, block_count, block_size)
        combined = (
            apply_blocks(main_blocks, padded, block_count, block_size)
            + even_weight[None, :] * coupled
            + odd_weight[None, :] * times_unit(coupled)
        )
        damping = jnp.where(depth_index >= floors[step], 0.5, 1.0).astype(jnp.float32)
        columns = (damping[:, None] * combined).astype(jnp.bfloat16)
    local_index = receivers - first_row
    selector = (local_index[:, None] == jnp.arange(rows_here, dtype=jnp.int32)[None, :]).astype(
        jnp.bfloat16
    )
    picked = jnp.dot(selector, columns, preferred_element_type=jnp.float32).astype(jnp.bfloat16)
    freq_here = columns.shape[1] // 2
    total_freq = frequencies.shape[0]
    factor = 1.0 / math.sqrt(total_freq)
    freq_values = lax.dynamic_slice_in_dim(
        frequencies, lax.axis_index("freq") * freq_here, freq_here, 0
    )
    basis_table = make_basis(freq_values, jnp.arange(NT, dtype=jnp.float32))
    owned_rows = summed_on_arrival(
        picked.astype(jnp.float32).astype(jnp.bfloat16), "depth", 0
    ).astype(jnp.bfloat16)
    owner_partial = jnp.dot(owned_rows, basis_table, preferred_element_type=jnp.float32)
    summed = summed_on_arrival_2(owner_partial, "freq", 1)
    return summed * factor


def solution(mesh):
    in_specs = (
        P("depth", "freq"),
        P("depth", None, None, None),
        P("depth", None, None, None),
        P("freq"),
        P(),
        P(),
        P(),
    )
    out_specs = P("depth", "freq")
    return jax.shard_map(local, mesh=mesh, in_specs=in_specs, out_specs=out_specs, check_vma=False)
```

profile of v0, /device:TPU:1, one launch (start us, length us, event | category | flops | bytes accessed | tf_op | source)
XLA Modules:
  0.0 527.0 jit_solution(9903431670786091757)
XLA Ops:
  16.4 6.9 %copy.22 = bf16[32,128,3,2,128]{4,1,3,0,2:T(8,128)(2,1)S(1)} copy(bf16[32,128,3,2,128]{4,3,2,1,0:T(2,128)(2,1)} %bitcast.287) | data formatting | bytes 12582912 | tf_op jit(solution)/shard_map/reshape | solution.py:54
  23.4 5.1 fusion.93
  42.0 5.8 %cosine_convert_fusion = (bf16[128,1,2048]{2,0,1:T(8,128)(2,1)}, bf16[128,1,2048]{2,0,1:T(8,128)(2,1)}) fusion(f32[128]{0:T(128)S(1)} %dynamic_slice.3), kind=kLoop, calls=%fused_computation.154 | loop fusion | flops 2883584 | bytes 1049088 | tf_op jit(solution)/shard_map/convert.1
  52.7 7.0 %bitcast_add_fusion = f32[32,256,256]{2,1,0:T(8,128)S(1)} fusion(f32[32,256,256]{2,1,0:T(8,128)} %fusion.93, f32[32,256,256]{1,2,0:T(8,128)} %fusion.86, bf16[32,128,256]{2,1,0:T(8,128)(2,1)S(1)} %bitcast.254, bf16[32,3,256,128]{3,2,0,1:T(8,128)(2,1)S(1)} %bitcast.202), kind=kOutput, calls=%fused_computation.2 | convolution fusion | flops 541065216 | bytes 29360128 | tf_op jit(solution)/shard_map/bij,bjc->bic/dot_general | solution.py:63
  88.8 10.6 %bitcast_add_fusion.2 = f32[32,256,256]{2,1,0:T(8,128)} fusion(f32[32,256,256]{2,1,0:T(8,128)} %fusion.82, f32[32,256,256]{1,2,0:T(8,128)} %fusion.75, bf16[32,128,256]{2,1,0:T(8,128)(2,1)S(1)} %bitcast.255, bf16[32,3,256,128]{3,2,0,1:T(8,128)(2,1)S(1)} %bitcast.190), kind=kOutput, calls=%fused_computation.4 | convolution fusion | flops 541065216 | bytes 29360128 | tf_op jit(solution)/shard_map/bij,bjc->bic/dot_general | solution.py:63
  99.4 6.2 %fusion.127 = (f32[32,128,256]{2,1,0:T(8,128)}, f32[32,128,256]{2,1,0:T(8,128)S(1)}) fusion(f32[32,256,256]{2,1,0:T(8,128)} %bitcast_add_fusion.2), kind=kLoop, calls=%fused_computation.195 | loop fusion | bytes 16777216 | tf_op jit(solution)/shard_map/slice | solution.py:69
  113.9 16.2 %fusion.16 = bf16[32,128,256]{2,1,0:T(8,128)(2,1)} fusion(f32[32,128,1]{2,1,0:T(8,128)} %bitcast.275, f32[32,128,255]{2,1,0:T(8,128)} %bitcast.243, f32[32,128,255]{2,1,0:T(8,128)} %bitcast.242, f32[32,128,1]{2,1,0:T(8,128)} %bitcast.274, f32[32,128,1]{2,1,0:T(8,128)} %bitcast.261, f32[32,128,255]{2,1,0:T(8,128)} %bitcast.229, ...), kind=kLoop, calls=%fused_computation.33 | loop fusion | flops 23068672 | bytes 35672320 | tf_op jit(solution)/shard_map/convert_element_type | solution.py:103
  130.1 6.3 %fusion.90 = f32[32,256,256]{1,2,0:T(8,128)} fusion(bf16[32,128,256]{2,1,0:T(8,128)(2,1)} %fusion.16, bf16[32,3,256,128]{3,2,0,1:T(8,128)(2,1)S(1)} %bitcast.203), kind=kOutput, calls=%fused_computation.142 | convolution fusion | flops 536870912 | bytes 12582912 | tf_op jit(solution)/shard_map/bij,bjc->bic/dot_general | solution.py:63
  136.4 10.6 %fusion.6 = bf16[4096,256]{1,0:T(8,128)(2,1)} fusion(f32[4096,1]{1,0:T(8,128)} %get-tuple-element.67, f32[4096,255]{1,0:T(8,128)} %get-tuple-element.69, f32[4096,255]{1,0:T(8,128)} %get-tuple-element.68, f32[4096,1]{1,0:T(8,128)} %get-tuple-element.66, f32[4096,1]{1,0:T(8,128)} %get-tuple-element.59, f32[4096,255]{1,0:T(8,128)S(1)} %copy-done.18, ...), kind=kLoop, calls=%fused_computation.20 | loop fusion | flops 17825792 | bytes 27283712 | tf_op jit(solution)/shard_map/convert_element_type | solution.py:103
  153.5 6.2 %fusion.79 = f32[32,256,256]{1,2,0:T(8,128)} fusion(bf16[32,128,256]{2,1,0:T(8,128)(2,1)} %fusion.16, bf16[32,3,256,128]{3,2,0,1:T(8,128)(2,1)S(1)} %bitcast.191), kind=kOutput, calls=%fused_computation.131 | convolution fusion | flops 536870912 | bytes 12582912 | tf_op jit(solution)/shard_map/bij,bjc->bic/dot_general | solution.py:63
  161.2 5.4 %fusion.87 = f32[32,256,256]{1,2,0:T(8,128)} fusion(bf16[32,128,256]{2,1,0:T(8,128)(2,1)S(1)} %bitcast.282, bf16[32,3,256,128]{3,2,0,1:T(8,128)(2,1)S(1)} %bitcast.204), kind=kOutput, calls=%fused_computation.139 | convolution fusion | flops 536870912 | bytes 12582912 | tf_op jit(solution)/shard_map/bij,bjc->bic/dot_general | solution.py:63
  167.4 8.6 %add_bitcast_fusion.4 = f32[32,256,256]{2,1,0:T(8,128)} fusion(f32[32,256,256]{1,2,0:T(8,128)} %fusion.87, f32[32,256,256]{1,2,0:T(8,128)S(1)} %bitcast.249, bf16[32,128,256]{2,1,0:T(8,128)(2,1)} %bitcast.256, bf16[32,3,256,128]{3,2,0,1:T(8,128)(2,1)S(1)} %bitcast.205), kind=kOutput, calls=%fused_computation.10 | convolution fusion | flops 541065216 | bytes 29360128 | tf_op jit(solution)/shard_map/bij,bjc->bic/dot_general | solution.py:63
  176.0 6.3 %fusion.126 = (f32[32,128,256]{2,1,0:T(8,128)}, f32[32,128,256]{2,1,0:T(8,128)S(1)}) fusion(f32[32,256,256]{2,1,0:T(8,128)} %add_bitcast_fusion.4), kind=kLoop, calls=%fused_computation.194 | loop fusion | bytes 16777216 | tf_op jit(solution)/shard_map/slice | solution.py:69
  206.3 10.3 %add_bitcast_fusion.5 = f32[32,256,256]{2,1,0:T(8,128)} fusion(f32[32,256,256]{1,2,0:T(8,128)} %fusion.76, f32[32,256,256]{1,2,0:T(8,128)} %fusion.79, bf16[32,128,256]{2,1,0:T(8,128)(2,1)S(1)} %bitcast.257, bf16[32,3,256,128]{3,2,0,1:T(8,128)(2,1)S(1)} %bitcast.193), kind=kOutput, calls=%fused_computation.11 | convolution fusion | flops 541065216 | bytes 29360128 | tf_op jit(solution)/shard_map/bij,bjc->bic/dot_general | solution.py:63
  216.6 6.2 %fusion.125 = (f32[32,128,256]{2,1,0:T(8,128)}, f32[32,128,256]{2,1,0:T(8,128)S(1)}) fusion(f32[32,256,256]{2,1,0:T(8,128)} %add_bitcast_fusion.5), kind=kLoop, calls=%fused_computation.193 | loop fusion | bytes 16777216 | tf_op jit(solution)/shard_map/slice | solution.py:69
  231.1 16.2 %fusion.37 = bf16[32,128,256]{2,1,0:T(8,128)(2,1)} fusion(f32[32,128,1]{2,1,0:T(8,128)} %bitcast.273, f32[32,128,255]{2,1,0:T(8,128)} %bitcast.241, f32[32,128,255]{2,1,0:T(8,128)} %bitcast.240, f32[32,128,1]{2,1,0:T(8,128)} %bitcast.272, f32[32,128,1]{2,1,0:T(8,128)} %bitcast.263, f32[32,128,255]{2,1,0:T(8,128)} %bitcast.231, ...), kind=kLoop, calls=%fused_computation.60 | loop fusion | flops 23068672 | bytes 35672320 | tf_op jit(solution)/shard_map/convert_element_type | solution.py:103
  247.3 6.3 %fusion.91 = f32[32,256,256]{1,2,0:T(8,128)} fusion(bf16[32,128,256]{2,1,0:T(8,128)(2,1)} %fusion.37, bf16[32,3,256,128]{3,2,0,1:T(8,128)(2,1)S(1)} %bitcast.206), kind=kOutput, calls=%fused_computation.143 | convolution fusion | flops 536870912 | bytes 12582912 | tf_op jit(solution)/shard_map/bij,bjc->bic/dot_general | solution.py:63
  253.6 11.0 %fusion.27 = bf16[4096,256]{1,0:T(8,128)(2,1)} fusion(f32[4096,1]{1,0:T(8,128)} %get-tuple-element.55, f32[4096,255]{1,0:T(8,128)} %get-tuple-element.57, f32[4096,255]{1,0:T(8,128)} %get-tuple-element.56, f32[4096,1]{1,0:T(8,128)} %get-tuple-element.54, f32[4096,1]{1,0:T(8,128)} %get-tuple-element.47, f32[4096,255]{1,0:T(8,128)S(1)} %copy-done.13, ...), kind=kLoop, calls=%fused_computation.47 | loop fusion | flops 17825792 | bytes 27283712 | tf_op jit(solution)/shard_map/convert_element_type | solution.py:103
  271.0 6.2 %fusion.80 = f32[32,256,256]{1,2,0:T(8,128)} fusion(bf16[32,128,256]{2,1,0:T(8,128)(2,1)} %fusion.37, bf16[32,3,256,128]{3,2,0,1:T(8,128)(2,1)S(1)} %bitcast.194), kind=kOutput, calls=%fused_computation.132 | convolution fusion | flops 536870912 | bytes 12582912 | tf_op jit(solution)/shard_map/bij,bjc->bic/dot_general | solution.py:63
  278.7 5.4 %fusion.88 = f32[32,256,256]{1,2,0:T(8,128)} fusion(bf16[32,128,256]{2,1,0:T(8,128)(2,1)S(1)} %bitcast.284, bf16[32,3,256,128]{3,2,0,1:T(8,128)(2,1)S(1)} %bitcast.207), kind=kOutput, calls=%fused_computation.140 | convolution fusion | flops 536870912 | bytes 12582912 | tf_op jit(solution)/shard_map/bij,bjc->bic/dot_general | solution.py:63
  284.9 8.6 %add_bitcast_fusion.2 = f32[32,256,256]{2,1,0:T(8,128)} fusion(f32[32,256,256]{1,2,0:T(8,128)} %fusion.88, f32[32,256,256]{1,2,0:T(8,128)S(1)} %bitcast.247, bf16[32,128,256]{2,1,0:T(8,128)(2,1)} %bitcast.258, bf16[32,3,256,128]{3,2,0,1:T(8,128)(2,1)S(1)} %bitcast.208), kind=kOutput, calls=%fused_computation.8 | convolution fusion | flops 541065216 | bytes 29360128 | tf_op jit(solution)/shard_map/bij,bjc->bic/dot_general | solution.py:63
  293.5 6.3 %fusion.124 = (f32[32,128,256]{2,1,0:T(8,128)}, f32[32,128,256]{2,1,0:T(8,128)S(1)}) fusion(f32[32,256,256]{2,1,0:T(8,128)} %add_bitcast_fusion.2), kind=kLoop, calls=%fused_computation.192 | loop fusion | bytes 16777216 | tf_op jit(solution)/shard_map/slice | solution.py:69
  324.0 10.3 %add_bitcast_fusion.3 = f32[32,256,256]{2,1,0:T(8,128)} fusion(f32[32,256,256]{1,2,0:T(8,128)} %fusion.77, f32[32,256,256]{1,2,0:T(8,128)} %fusion.80, bf16[32,128,256]{2,1,0:T(8,128)(2,1)S(1)} %bitcast.259, bf16[32,3,256,128]{3,2,0,1:T(8,128)(2,1)S(1)} %bitcast.196), kind=kOutput, calls=%fused_computation.9 | convolution fusion | flops 541065216 | bytes 29360128 | tf_op jit(solution)/shard_map/bij,bjc->bic/dot_general | solution.py:63
  334.3 6.2 %fusion.123 = (f32[32,128,256]{2,1,0:T(8,128)}, f32[32,128,256]{2,1,0:T(8,128)S(1)}) fusion(f32[32,256,256]{2,1,0:T(8,128)} %add_bitcast_fusion.3), kind=kLoop, calls=%fused_computation.191 | loop fusion | bytes 16777216 | tf_op jit(solution)/shard_map/slice | solution.py:69
  348.8 16.2 %fusion.58 = bf16[32,128,256]{2,1,0:T(8,128)(2,1)} fusion(f32[32,128,1]{2,1,0:T(8,128)} %bitcast.277, f32[32,128,255]{2,1,0:T(8,128)} %bitcast.245, f32[32,128,255]{2,1,0:T(8,128)} %bitcast.244, f32[32,128,1]{2,1,0:T(8,128)} %bitcast.276, f32[32,128,1]{2,1,0:T(8,128)} %bitcast.267, f32[32,128,255]{2,1,0:T(8,128)} %bitcast.235, ...), kind=kLoop, calls=%fused_computation.87 | loop fusion | flops 23068672 | bytes 35672320 | tf_op jit(solution)/shard_map/convert_element_type | solution.py:103
  365.1 6.3 %fusion.92 = f32[32,256,256]{1,2,0:T(8,128)} fusion(bf16[32,128,256]{2,1,0:T(8,128)(2,1)} %fusion.58, bf16[32,3,256,128]{3,2,0,1:T(8,128)(2,1)S(1)} %bitcast.209), kind=kOutput, calls=%fused_computation.144 | convolution fusion | flops 536870912 | bytes 12582912 | tf_op jit(solution)/shard_map/bij,bjc->bic/dot_general | solution.py:63
  371.4 10.8 %fusion.48 = bf16[4096,256]{1,0:T(8,128)(2,1)} fusion(f32[4096,1]{1,0:T(8,128)} %get-tuple-element.43, f32[4096,255]{1,0:T(8,128)} %get-tuple-element.45, f32[4096,255]{1,0:T(8,128)} %get-tuple-element.44, f32[4096,1]{1,0:T(8,128)} %get-tuple-element.42, f32[4096,1]{1,0:T(8,128)} %get-tuple-element.35, f32[4096,255]{1,0:T(8,128)S(1)} %copy-done.20, ...), kind=kLoop, calls=%fused_computation.74 | loop fusion | flops 17825792 | bytes 27283712 | tf_op jit(solution)/shard_map/convert_element_type | solution.py:103
  398.3 10.9 %add_bitcast_fusion = f32[32,256,256]{2,1,0:T(8,128)} fusion(f32[32,256,256]{1,2,0:T(8,128)} %fusion.89, f32[32,256,256]{1,2,0:T(8,128)} %fusion.92, bf16[32,128,256]{2,1,0:T(8,128)(2,1)} %bitcast.252, bf16[32,3,256,128]{3,2,0,1:T(8,128)(2,1)S(1)} %bitcast.211), kind=kOutput, calls=%fused_computation.6 | convolution fusion | flops 541065216 | bytes 29360128 | tf_op jit(solution)/shard_map/bij,bjc->bic/dot_general | solution.py:63
  409.3 6.2 %fusion.122 = (f32[32,128,256]{2,1,0:T(8,128)}, f32[32,128,256]{2,1,0:T(8,128)S(1)}) fusion(f32[32,256,256]{2,1,0:T(8,128)} %add_bitcast_fusion), kind=kLoop, calls=%fused_computation.190 | loop fusion | bytes 16777216 | tf_op jit(solution)/shard_map/slice | solution.py:69
  439.5 8.0 %add_bitcast_fusion.1 = f32[32,256,256]{2,1,0:T(8,128)} fusion(f32[32,256,256]{1,2,0:T(8,128)} %fusion.78, f32[32,256,256]{1,2,0:T(8,128)S(1)} %fusion.81, bf16[32,128,256]{2,1,0:T(8,128)(2,1)S(1)} %bitcast.253, bf16[32,3,256,128]{3,2,0,1:T(8,128)(2,1)S(1)} %bitcast.199), kind=kOutput, calls=%fused_computation.7 | convolution fusion | flops 541065216 | bytes 29360128 | tf_op jit(solution)/shard_map/bij,bjc->bic/dot_general | solution.py:63
  459.8 7.7 %fusion.69 = bf16[4096,256]{1,0:T(8,128)(2,1)S(1)} fusion(f32[4096,1]{1,0:T(8,128)} %get-tuple-element.31, f32[4096,255]{1,0:T(8,128)} %get-tuple-element.33, f32[4096,255]{1,0:T(8,128)S(1)} %get-tuple-element.32, f32[4096,1]{1,0:T(8,128)} %get-tuple-element.30, f32[4096,1]{1,0:T(8,128)} %get-tuple-element.23, f32[4096,255]{1,0:T(8,128)S(1)} %copy-done.42, ...), kind=kLoop, calls=%fused_computation.101 | loop fusion | flops 17825792 | bytes 27283712 | tf_op jit(solution)/shard_map/convert_element_type | solution.py:103
  480.1 45.7 %all_to_all.10 = f32[64,256,32]{1,2,0:T(8,128)S(1)} all-to-all(f32[64,256,32]{1,2,0:T(8,128)S(1)} %copy.27), channel_id=1, replica_groups=mesh['freq'=64,'depth'=2] {'freq'}, dimensions={0} | all-to-all | bytes 4194304 | tf_op jit(solution)/shard_map/all_to_all | solution.py:42
  (222 shorter events, 220.0 us)
Async XLA Ops:
  0.0 33.2 %copy-start = (f32[256]{0:T(256)S(1)}, f32[256]{0:T(256)}, u32[]{:S(2)}) copy-start(f32[256]{0:T(256)} %param.12) | copy-start | bytes 3076
  0.9 46.9 %collective-permute-start = (bf16[128,256]{1,0:T(8,128)(2,1)S(1)}, bf16[128,256]{1,0:T(8,128)(2,1)S(1)}, u32[]{:S(2)}, u32[]{:S(2)}) collective-permute-start(bf16[128,256]{1,0:T(8,128)(2,1)S(1)} %get-tuple-element.85), channel_id=1, source_target_pairs={{0,1},{2,3},{4,5},{6,7},{8,9},{10,11},{12,13},{14,15},{16,17},{18,... | collective-permute-start | bytes 196616 | tf_op jit(solution)/shard_map/ppermute | solution.py:20
  5.3 42.5 %collective-permute-start.1 = (bf16[128,256]{1,0:T(8,128)(2,1)S(1)}, bf16[128,256]{1,0:T(8,128)(2,1)S(1)}, u32[]{:S(2)}, u32[]{:S(2)}) collective-permute-start(bf16[128,256]{1,0:T(8,128)(2,1)S(1)} %get-tuple-element.84), channel_id=1, source_target_pairs={{1,0},{3,2},{5,4},{7,6},{9,8},{11,10},{13,12},{15,14},{17,16},{19,... | collective-permute-start | bytes 196616 | tf_op jit(solution)/shard_map/ppermute | solution.py:22
  16.4 7.0 %copy-start.3 = (bf16[32,128,3,2,128]{4,1,3,0,2:T(8,128)(2,1)}, bf16[32,128,3,2,128]{4,1,3,0,2:T(8,128)(2,1)S(1)}, u32[]{:S(2)}) copy-start(bf16[32,128,3,2,128]{4,1,3,0,2:T(8,128)(2,1)S(1)} %copy.23) | copy-start | bytes 18874372
  16.4 7.0 %copy-start.21 = (bf16[4096,256]{1,0:T(8,128)(2,1)S(1)}, bf16[4096,256]{1,0:T(8,128)(2,1)}, u32[]{:S(2)}) copy-start(bf16[4096,256]{1,0:T(8,128)(2,1)} %param.9) | copy-start | bytes 6291460
  28.6 11.8 %copy-start.56 = (s32[512]{0:T(512)S(1)}, s32[512]{0:T(512)}, u32[]{:S(2)}) copy-start(s32[512]{0:T(512)} %param.14) | copy-start | bytes 6148
  41.1 7.0 %copy-start.4 = (bf16[32,128,3,2,128]{4,1,3,0,2:T(8,128)(2,1)S(1)}, bf16[32,128,3,2,128]{4,1,3,0,2:T(8,128)(2,1)}, u32[]{:S(2)}) copy-start(bf16[32,128,3,2,128]{4,1,3,0,2:T(8,128)(2,1)} %copy-done.3) | copy-start | bytes 18874372
  67.6 6.4 %copy-start.43 = (f32[32,128,256]{2,1,0:T(8,128)S(1)}, f32[32,128,256]{2,1,0:T(8,128)}, u32[]{:S(2)}) copy-start(f32[32,128,256]{2,1,0:T(8,128)} %get-tuple-element.20) | copy-start | bytes 12582916
  73.9 10.3 %slice-start = ((s8[6291456]{0:T(1024)(128)(4,1)}), s8[4194304]{0:T(1024)(128)(4,1)S(1)}, s32[]{:S(2)}) async-start(s8[6291456]{0:T(1024)(128)(4,1)} %bitcast.187), calls=%async_computation.2 | async-start | bytes 8388608
  76.9 7.2 %slice-start.1 = ((s8[6291456]{0:T(1024)(128)(4,1)}), s8[2097152]{0:T(1024)(128)(4,1)S(1)}, s32[]{:S(2)}) async-start(s8[6291456]{0:T(1024)(128)(4,1)} %bitcast.187), calls=%async_computation.3 | async-start | bytes 4194304
  130.0 6.3 %copy-start.17 = (f32[4096,255]{1,0:T(8,128)S(1)}, f32[4096,255]{1,0:T(8,128)}, u32[]{:S(2)}) copy-start(f32[4096,255]{1,0:T(8,128)} %get-tuple-element.60) | copy-start | bytes 12533764
  130.0 6.3 %copy-start.18 = (f32[4096,255]{1,0:T(8,128)S(1)}, f32[4096,255]{1,0:T(8,128)}, u32[]{:S(2)}) copy-start(f32[4096,255]{1,0:T(8,128)} %get-tuple-element.61) | copy-start | bytes 12533764
  147.9 11.8 %collective-permute-start.2 = (bf16[128,256]{1,0:T(8,128)(2,1)S(1)}, bf16[128,256]{1,0:T(8,128)(2,1)S(1)}, u32[]{:S(2)}, u32[]{:S(2)}) collective-permute-start(bf16[128,256]{1,0:T(8,128)(2,1)S(1)} %get-tuple-element.81), channel_id=1, source_target_pairs={{0,1},{2,3},{4,5},{6,7},{8,9},{10,11},{12,13},{14,15},{16,17},{18,... | collective-permute-start | bytes 196616 | tf_op jit(solution)/shard_map/ppermute | solution.py:20
  151.9 7.8 %copy-start.46 = (bf16[4096,256]{1,0:T(8,128)(2,1)S(1)}, bf16[4096,256]{1,0:T(8,128)(2,1)}, u32[]{:S(2)}) copy-start(bf16[4096,256]{1,0:T(8,128)(2,1)} %fusion.6) | copy-start | bytes 6291460
  151.9 7.8 %collective-permute-start.3 = (bf16[128,256]{1,0:T(8,128)(2,1)S(1)}, bf16[128,256]{1,0:T(8,128)(2,1)S(1)}, u32[]{:S(2)}, u32[]{:S(2)}) collective-permute-start(bf16[128,256]{1,0:T(8,128)(2,1)S(1)} %get-tuple-element.80), channel_id=1, source_target_pairs={{1,0},{3,2},{5,4},{7,6},{9,8},{11,10},{13,12},{15,14},{17,16},{19,... | collective-permute-start | bytes 196616 | tf_op jit(solution)/shard_map/ppermute | solution.py:22
  159.7 7.0 %slice-start.4 = ((s8[8388608]{0:T(1024)(128)(4,1)}), s8[4194304]{0:T(1024)(128)(4,1)S(1)}, s32[]{:S(2)}) async-start(s8[8388608]{0:T(1024)(128)(4,1)} %bitcast.248), calls=%async_computation.6 | async-start | bytes 8388608
  161.2 6.2 %slice-start.5 = ((s8[8388608]{0:T(1024)(128)(4,1)}), s8[4194304]{0:T(1024)(128)(4,1)S(1)}, s32[]{:S(2)}) async-start(s8[8388608]{0:T(1024)(128)(4,1)} %bitcast.248), calls=%async_computation.7 | async-start | bytes 8388608
  247.3 6.3 %copy-start.12 = (f32[4096,255]{1,0:T(8,128)S(1)}, f32[4096,255]{1,0:T(8,128)}, u32[]{:S(2)}) copy-start(f32[4096,255]{1,0:T(8,128)} %get-tuple-element.48) | copy-start | bytes 12533764
  247.3 6.3 %copy-start.13 = (f32[4096,255]{1,0:T(8,128)S(1)}, f32[4096,255]{1,0:T(8,128)}, u32[]{:S(2)}) copy-start(f32[4096,255]{1,0:T(8,128)} %get-tuple-element.49) | copy-start | bytes 12533764
  247.3 6.3 %copy-start.54 = (f32[4096]{0:T(1024)S(1)}, f32[4096]{0:T(1024)}, u32[]{:S(2)}) copy-start(f32[4096]{0:T(1024)} %get-tuple-element.98) | copy-start | bytes 49156
  265.5 11.6 %collective-permute-start.4 = (bf16[128,256]{1,0:T(8,128)(2,1)S(1)}, bf16[128,256]{1,0:T(8,128)(2,1)S(1)}, u32[]{:S(2)}, u32[]{:S(2)}) collective-permute-start(bf16[128,256]{1,0:T(8,128)(2,1)S(1)} %get-tuple-element.77), channel_id=1, source_target_pairs={{0,1},{2,3},{4,5},{6,7},{8,9},{10,11},{12,13},{14,15},{16,17},{18,... | collective-permute-start | bytes 196616 | tf_op jit(solution)/shard_map/ppermute | solution.py:20
  269.5 7.6 %copy-start.47 = (bf16[4096,256]{1,0:T(8,128)(2,1)S(1)}, bf16[4096,256]{1,0:T(8,128)(2,1)}, u32[]{:S(2)}) copy-start(bf16[4096,256]{1,0:T(8,128)(2,1)} %fusion.27) | copy-start | bytes 6291460
  269.5 7.6 %collective-permute-start.5 = (bf16[128,256]{1,0:T(8,128)(2,1)S(1)}, bf16[128,256]{1,0:T(8,128)(2,1)S(1)}, u32[]{:S(2)}, u32[]{:S(2)}) collective-permute-start(bf16[128,256]{1,0:T(8,128)(2,1)S(1)} %get-tuple-element.76), channel_id=1, source_target_pairs={{1,0},{3,2},{5,4},{7,6},{9,8},{11,10},{13,12},{15,14},{17,16},{19,... | collective-permute-start | bytes 196616 | tf_op jit(solution)/shard_map/ppermute | solution.py:22
  277.1 7.0 %slice-start.2 = ((s8[8388608]{0:T(1024)(128)(4,1)}), s8[4194304]{0:T(1024)(128)(4,1)S(1)}, s32[]{:S(2)}) async-start(s8[8388608]{0:T(1024)(128)(4,1)} %bitcast.246), calls=%async_computation.4 | async-start | bytes 8388608
  365.0 6.3 %copy-start.19 = (f32[4096,255]{1,0:T(8,128)S(1)}, f32[4096,255]{1,0:T(8,128)}, u32[]{:S(2)}) copy-start(f32[4096,255]{1,0:T(8,128)} %get-tuple-element.36) | copy-start | bytes 12533764
  365.0 6.3 %copy-start.20 = (f32[4096,255]{1,0:T(8,128)S(1)}, f32[4096,255]{1,0:T(8,128)}, u32[]{:S(2)}) copy-start(f32[4096,255]{1,0:T(8,128)} %get-tuple-element.37) | copy-start | bytes 12533764
  365.0 6.3 %copy-start.52 = (f32[4096]{0:T(1024)S(1)}, f32[4096]{0:T(1024)}, u32[]{:S(2)}) copy-start(f32[4096]{0:T(1024)} %get-tuple-element.97) | copy-start | bytes 49156
  383.1 8.3 %collective-permute-start.6 = (bf16[128,256]{1,0:T(8,128)(2,1)S(1)}, bf16[128,256]{1,0:T(8,128)(2,1)S(1)}, u32[]{:S(2)}, u32[]{:S(2)}) collective-permute-start(bf16[128,256]{1,0:T(8,128)(2,1)S(1)} %get-tuple-element.73), channel_id=1, source_target_pairs={{0,1},{2,3},{4,5},{6,7},{8,9},{10,11},{12,13},{14,15},{16,17},{18,... | collective-permute-start | bytes 196616 | tf_op jit(solution)/shard_map/ppermute | solution.py:20
  387.1 5.1 collective-permute-start.7
  459.8 7.7 %copy-start.57 = (s32[512]{0:T(512)S(1)}, s32[512]{0:T(512)}, u32[]{:S(2)}) copy-start(s32[512]{0:T(512)} %broadcast_subtract_fusion) | copy-start | bytes 6148
  469.8 7.7 %all-to-all-start = ((bf16[2,256,256]{2,1,0:T(8,128)(2,1)}), bf16[2,256,256]{2,1,0:T(8,128)(2,1)S(1)}, u32[]{:S(2)}, u32[]{:S(2)}) async-start(bf16[2,256,256]{2,1,0:T(8,128)(2,1)} %bitcast.89), calls=%async_computation | async-start | bytes 524288 | tf_op jit(solution)/shard_map/all_to_all | solution.py:36
  478.8 47.7 %copy-start.1 = (f32[256]{0:T(256)S(1)}, f32[256]{0:T(256)}, u32[]{:S(2)}) copy-start(f32[256]{0:T(256)} %param.12) | copy-start | bytes 3076
  (41 other events, 163.3 us)
where the time goes:
time: 532 us; the launch traced here: 527 us
  local copies, waits for them, and re-layouts  170 us (32%)
  matrix products  160 us (30%)
  other arithmetic  122 us (23%)
  blocking collectives  45.7 us (9%)
  starting transfers between devices  25.8 us (5%)
    dot_general x24, matrix products, apply_blocks(): jnp.einsum('bij,bjc->bic', ordered[:, offset], stacked[offset:offset + bl...  156 us
    convert_element_type x7, other arithmetic, local(): columns = (damping[:, None] * combined).astype(jnp.bfloat16)  88.7 us
    slice x24, local copies, waits for them, and re-layouts, times_unit(): lower = jnp.roll(values, 1, axis=1)  74.9 us
    all_to_all x1, blocking collectives, summed_on_arrival_2(): lax.all_to_all(parts, axis, split_axis=0, concat_axis=0, tiled=True)  45.7 us
    slice x8, local copies, waits for them, and re-layouts, apply_blocks(): real_part = product[:, :block_size].reshape(block_count * block_size, width)  44.5 us
    unnamed x128, local copies, waits for them, and re-layouts  25.3 us
    ppermute x4, starting transfers between devices, padded_2(): lax.ppermute(tail, axis, [(i, (i + 1) % count) for i in range(ends)])  16.3 us
    add x4, other arithmetic, apply_blocks(): return real_part + times_unit(imag_part)  14.6 us
  transfers between devices with their start and end apart: 9, of which 2 were waited for; matrix products, arithmetic and copies ran while one was open for 11% of the time, Pallas kernels for 0%

commit v1 on v0

v1 whole, which is shorter than its diff:
```python
import functools
import math

import jax
import jax.numpy as jnp
from jax import lax
from jax.experimental import pallas as pl
from jax.experimental.pallas import tpu as pltpu
from jax.sharding import PartitionSpec as P

NT = 2048
STEPS = 4
BS = 128
MESH = pl.DeviceIdType.MESH
F32 = jnp.float32
BF16 = jnp.bfloat16


def iota(shape, dim):
    return lax.broadcasted_iota(jnp.int32, shape, dim)


def dot(a, b):
    return jnp.dot(a, b, preferred_element_type=F32)


def dot_nt(a, b):
    return lax.dot_general(a, b, (((1,), (1,)), ((), ())), preferred_element_type=F32)


def times_unit(x):
    return jnp.concatenate([-x[:, BS:], x[:, :BS]], axis=1)


def march_kernel(
    nb,
    unroll,
    field_hbm,
    main_hbm,
    side_hbm,
    coupling,
    receivers,
    floors,
    picked_out,
    raw_field,
    raw_main,
    raw_side,
    ops,
    state,
    final,
    selector,
    recv_col,
    weights,
    split,
    order,
    halo,
    theirs,
    arrived,
    field_sem,
    main_sem,
    side_sem,
    halo_send,
    halo_recv,
    pick_send,
    pick_recv,
):
    depth = lax.axis_index("depth")
    other = 1 - depth
    width = 2 * BS
    rows_here = nb * BS
    first_row = depth * rows_here
    half = theirs.shape[0]

    def block_at(i):
        return jnp.where(depth == 0, i, nb - 1 - i)

    edge = block_at(nb - 1)
    halo_slot = jnp.where(depth == 0, nb + 1, 0)

    def field_copy(b):
        return pltpu.make_async_copy(
            field_hbm.at[pl.ds(pl.multiple_of(b * BS, BS), BS), :],
            raw_field.at[pl.ds(pl.multiple_of(b * BS, BS), BS), :],
            field_sem.at[b],
        )

    def op_copy(hbm, raw, sem, b):
        rows = 6 * BS
        return pltpu.make_async_copy(
            hbm.at[pl.ds(pl.multiple_of(b * rows, rows), rows), :],
            raw.at[pl.ds(pl.multiple_of(b * rows, rows), rows), :],
            sem.at[b],
        )

    field_copy(edge).start()

    @pl.loop(0, nb - 1)
    def _(i):
        field_copy(block_at(i)).start()

    @pl.loop(0, nb)
    def _(i):
        op_copy(main_hbm, raw_main, main_sem, block_at(i)).start()
        op_copy(side_hbm, raw_side, side_sem, block_at(i)).start()

    barrier = pltpu.get_barrier_semaphore()
    pl.semaphore_signal(barrier, inc=1, device_id={"depth": other}, device_id_type=MESH)

    row, col = iota((width, width), 0), iota((width, width), 1)
    wanted = jnp.where(col < BS, 2 * col, 2 * (col - BS) + 1)
    split[...] = jnp.where(row == wanted, 1.0, 0.0).astype(BF16)
    row, col = iota((192, 192), 0), iota((192, 192), 1)
    order[...] = jnp.where(col == 6 * (row & 31) + (row >> 5), 1.0, 0.0).astype(BF16)
    split_f32 = split[...].astype(F32)
    weights[...] = jnp.dot(
        jnp.broadcast_to(coupling[...], (8, width)),
        split_f32,
        precision=lax.Precision.HIGHEST,
        preferred_element_type=F32,
    )
    spots = receivers[...].astype(F32)
    for g in range(receivers.shape[0]):
        tile = jnp.broadcast_to(spots[g : g + 1, :], (BS, BS))
        recv_col[g * BS : (g + 1) * BS, :] = tile.T
    empty = jnp.zeros((2 * BS, width), BF16)
    for par in range(2):
        state[par, 0 : 2 * BS, :] = empty
        state[par, (nb + 1) * 2 * BS : (nb + 2) * 2 * BS, :] = empty

    def put(par, slot, x):
        start = pl.multiple_of(slot * 2 * BS, 2 * BS)
        state[par, pl.ds(start, BS), :] = x
        state[par, pl.ds(start + BS, BS), :] = times_unit(x)

    def halo_copy(step, src):
        return pltpu.make_async_remote_copy(
            src_ref=src,
            dst_ref=halo.at[step],
            send_sem=halo_send.at[step],
            recv_sem=halo_recv.at[step],
            device_id={"depth": other},
            device_id_type=MESH,
        )

    field_copy(edge).wait()
    pl.semaphore_wait(barrier, 1)
    edge_rows = pl.ds(pl.multiple_of(edge * BS, BS), BS)
    first_halo = halo_copy(0, raw_field.at[edge_rows, :])
    first_halo.start()

    def deinterleave(b):
        rows = pl.ds(pl.multiple_of(b * BS, BS), BS)
        put(0, b + 1, dot(raw_field[rows, :], split[...]).astype(BF16))

    @pl.loop(0, (nb - unroll) // unroll)
    def _(t):
        for u in range(unroll):
            field_copy(block_at(t * unroll + u)).wait()
        for u in range(unroll):
            deinterleave(block_at(t * unroll + u))

    for u in range(unroll - 1):
        field_copy(block_at(nb - unroll + u)).wait()
    for u in range(unroll):
        deinterleave(block_at(nb - unroll + u))

    def bring_in(b):
        base = pl.multiple_of(b * 6 * BS, 6 * BS)
        dest = pl.multiple_of(b * 2 * BS, 2 * BS)
        for q in range(4):
            part = pl.ds(base + 192 * q, 192)
            both = jnp.concatenate([raw_main[part, :], raw_side[part, :]], axis=1)
            sorted_rows = dot(order[...], both).astype(BF16)
            for kc in range(6):
                tile = sorted_rows[32 * kc : 32 * kc + 32, :]
                lanes = slice(kc * BS, (kc + 1) * BS)
                ops[pl.ds(dest + 32 * q, 32), lanes] = tile[:, :BS]
                ops[pl.ds(dest + BS + 32 * q, 32), lanes] = tile[:, BS:]

    def select(b):
        target = (first_row + b * BS).astype(F32)
        lane = iota((2 * half, BS), 1).astype(F32) + target
        lanes = pl.ds(pl.multiple_of(b * BS, BS), BS)
        selector[:, lanes] = jnp.where(recv_col[...] == lane, 1.0, 0.0).astype(BF16)

    def advance(step, par, b):
        lhs = ops[pl.ds(pl.multiple_of(b * 2 * BS, 2 * BS), 2 * BS), :]
        rhs = state[par, pl.ds(pl.multiple_of(b * 2 * BS, 2 * BS), 6 * BS), :]
        product = dot(lhs, rhs)
        main, side = product[:BS], product[BS:]
        w_real, w_imag = weights[0:1, :BS], weights[0:1, BS:]
        side_real, side_imag = side[:, :BS], side[:, BS:]
        real = main[:, :BS] + (w_real * side_real - w_imag * side_imag)
        imag = main[:, BS:] + (w_real * side_imag + w_imag * side_real)
        depth_index = first_row + b * BS + iota((BS, BS), 0)
        damping = jnp.where(depth_index >= floors[step], 0.5, 1.0).astype(F32)
        return jnp.concatenate([damping * real, damping * imag], axis=1).astype(BF16)

    trips = nb // unroll

    @pl.loop(0, trips)
    def _(t):
        @pl.when(t == trips - 1)
        def _():
            first_halo.wait()
            put(0, halo_slot, dot(halo[0], split[...]).astype(BF16))

        for u in range(unroll):
            b = block_at(t * unroll + u)
            op_copy(main_hbm, raw_main, main_sem, b).wait()
            op_copy(side_hbm, raw_side, side_sem, b).wait()
        for u in range(unroll):
            b = block_at(t * unroll + u)
            bring_in(b)
            select(b)
        for u in range(unroll):
            b = block_at(t * unroll + u)
            put(1, b + 1, advance(0, 0, b))

    def edge_of(par):
        return state.at[par, pl.ds(pl.multiple_of((edge + 1) * 2 * BS, 2 * BS), BS), :]

    halo_copy(1, edge_of(1)).start()

    @pl.loop(1, STEPS - 1)
    def _(step):
        par = step & 1

        @pl.loop(0, trips)
        def _(t):
            @pl.when(t == trips - 1)
            def _():
                halo_copy(step, edge_of(par)).wait()
                put(par, halo_slot, halo[step])

            for u in range(unroll):
                b = block_at(t * unroll + u)
                put(1 - par, b + 1, advance(step, par, b))

        halo_copy(step + 1, edge_of(1 - par)).start()

    par = (STEPS - 1) & 1

    @pl.loop(0, trips)
    def _(t):
        @pl.when(t == trips - 1)
        def _():
            halo_copy(STEPS - 1, edge_of(par)).wait()
            put(par, halo_slot, halo[STEPS - 1])

        for u in range(unroll):
            b = block_at(t * unroll + u)
            final[pl.ds(pl.multiple_of(b * BS, BS), BS), :] = advance(STEPS - 1, par, b)

    def pick(owner):
        rows = pl.ds(pl.multiple_of(owner * half, half), half)
        return dot(selector[rows, :], final[...]).astype(BF16)

    theirs[...] = pick(other)
    swap = pltpu.make_async_remote_copy(
        src_ref=theirs,
        dst_ref=arrived,
        send_sem=pick_send,
        recv_sem=pick_recv,
        device_id={"depth": other},
        device_id_type=MESH,
    )
    swap.start()
    mine = pick(depth)
    swap.wait()
    picked_out[...] = mine + arrived[...]


def poly_coeffs():
    import numpy as np

    x = np.cos(np.pi * (np.arange(400) + 0.5) / 400) * 0.125 + 0.125
    y = np.sqrt(x)
    cheb_c = np.polynomial.chebyshev.Chebyshev.fit(x, np.cos(2 * np.pi * y), 8, domain=[0, 0.25])
    cheb_s = np.polynomial.chebyshev.Chebyshev.fit(x, np.sin(2 * np.pi * y) / y, 8, domain=[0, 0.25])
    to = np.polynomial.polynomial.Polynomial
    return (
        [float(v) for v in cheb_c.convert(kind=to).coef],
        [float(v) for v in cheb_s.convert(kind=to).coef],
    )


COS_COEFFS, SIN_COEFFS = poly_coeffs()


def horner(coeffs, z):
    total = jnp.full_like(z, coeffs[-1])
    for c in reversed(coeffs[:-1]):
        total = total * z + c
    return total


def cos_sin(turns):
    r = turns - jnp.floor(turns + 0.5)
    z = r * r
    return horner(COS_COEFFS, z), r * horner(SIN_COEFFS, z)


def synth_kernel(
    chips,
    factor,
    picked,
    frequencies,
    out,
    partner,
    basis,
    near,
    far,
    sums,
    inbox,
    pair_send,
    pair_recv,
    send_sem,
    recv_sem,
):
    me = lax.axis_index("freq")
    chip, core = me // 2, me % 2
    span = NT // (2 * chips)
    rows = picked.shape[0]

    barrier = pltpu.get_barrier_semaphore()
    mate = 2 * chip + (1 - core)
    pl.semaphore_signal(barrier, inc=1, device_id={"freq": mate}, device_id_type=MESH)

    @pl.loop(1, chips)
    def _(k):
        peer = 2 * ((chip + k) % chips) + core
        pl.semaphore_signal(barrier, inc=1, device_id={"freq": peer}, device_id_type=MESH)

    pl.semaphore_wait(barrier, chips)

    swap = pltpu.make_async_remote_copy(
        src_ref=picked,
        dst_ref=partner,
        send_sem=pair_send,
        recv_sem=pair_recv,
        device_id={"freq": mate},
        device_id_type=MESH,
    )
    swap.start()

    own_f = frequencies[pl.ds(me, 1), :]
    mate_f = frequencies[pl.ds(mate, 1), :]
    freq = jnp.concatenate([own_f, mate_f], axis=1)
    scale = 1.0 / NT
    step_in = iota((span, 2 * BS), 0).astype(F32)
    cos_b, sin_b = cos_sin(freq * step_in * scale)
    start = ((2 * iota((chips, 2 * BS), 0) + core) * span).astype(F32)
    cos_a, sin_a = cos_sin(freq * start * scale)
    near[0], near[1] = cos_b, sin_b
    far[0], far[1] = cos_a, sin_a

    @pl.loop(0, chips)
    def _(j):
        ca, sa = far[0, pl.ds(j, 1), :], far[1, pl.ds(j, 1), :]
        cb, sb = near[0], near[1]
        real = (ca * cb - sa * sb).astype(BF16)
        imag = (-(sa * cb + ca * sb)).astype(BF16)
        place = pl.ds(pl.multiple_of(j * span, span), span)
        basis[place, 0:BS] = real[:, :BS]
        basis[place, BS : 2 * BS] = imag[:, :BS]
        basis[place, 2 * BS : 3 * BS] = real[:, BS:]
        basis[place, 3 * BS : 4 * BS] = imag[:, BS:]

    swap.wait()

    def outgoing(j):
        return pltpu.make_async_remote_copy(
            src_ref=sums.at[j],
            dst_ref=inbox.at[chip],
            send_sem=send_sem.at[j],
            recv_sem=recv_sem.at[chip],
            device_id={"freq": 2 * j + core},
            device_id_type=MESH,
        )

    def incoming(j):
        return pltpu.make_async_remote_copy(
            src_ref=sums.at[chip],
            dst_ref=inbox.at[j],
            send_sem=send_sem.at[chip],
            recv_sem=recv_sem.at[j],
            device_id={"freq": 2 * j + core},
            device_id_type=MESH,
        )

    batch = min(8, chips)

    @pl.loop(0, chips // batch)
    def _(g):
        group = (chip // batch + g) % (chips // batch)
        place = pl.ds(pl.multiple_of(group * batch * span, batch * span), batch * span)
        part = dot_nt(basis[place, : 2 * BS], picked[...]) + dot_nt(
            basis[place, 2 * BS :], partner[...]
        )
        part = (part * factor).astype(BF16)
        for u in range(batch):
            sums[group * batch + u] = part[u * span : (u + 1) * span, :]
        for u in range(batch):
            j = group * batch + u

            @pl.when(j != chip)
            def _():
                outgoing(j).start()

    inbox[chip] = sums[chip]

    @pl.loop(1, chips)
    def _(k):
        incoming((chip + k) % chips).wait_recv()

    total = inbox[0].astype(F32)
    for j in range(1, chips):
        total = total + inbox[j].astype(F32)
    out[...] = total

    @pl.loop(1, chips)
    def _(k):
        outgoing((chip + k) % chips).wait_send()


def local(pressure_field, block_main, block_coupled, coupling, frequencies, receivers, floors):
    rows_here, width = pressure_field.shape
    nb = rows_here // BS
    unroll = min(8, nb // 2)
    count = receivers.shape[0]
    half = count // 2
    any_space = pl.BlockSpec(memory_space=pl.ANY)
    vmem = pl.BlockSpec(memory_space=pltpu.VMEM)
    smem = pl.BlockSpec(memory_space=pltpu.SMEM)
    dma = pltpu.SemaphoreType.DMA
    picked = pl.pallas_call(
        functools.partial(march_kernel, nb, unroll),
        out_shape=jax.ShapeDtypeStruct((half, width), BF16),
        in_specs=[any_space, any_space, any_space, vmem, vmem, smem],
        out_specs=vmem,
        scratch_shapes=[
            pltpu.VMEM((rows_here, width), BF16),
            pltpu.VMEM((rows_here * 6, BS), BF16),
            pltpu.VMEM((rows_here * 6, BS), BF16),
            pltpu.VMEM((nb * 2 * BS, 6 * BS), BF16),
            pltpu.VMEM((2, (nb + 2) * 2 * BS, width), BF16),
            pltpu.VMEM((rows_here, width), BF16),
            pltpu.VMEM((count, rows_here), BF16),
            pltpu.VMEM((count, BS), F32),
            pltpu.VMEM((8, width), F32),
            pltpu.VMEM((width, width), BF16),
            pltpu.VMEM((192, 192), BF16),
            pltpu.VMEM((STEPS, BS, width), BF16),
            pltpu.VMEM((half, width), BF16),
            pltpu.VMEM((half, width), BF16),
            dma((nb,)),
            dma((nb,)),
            dma((nb,)),
            dma((STEPS,)),
            dma((STEPS,)),
            dma,
            dma,
        ],
        compiler_params=pltpu.CompilerParams(
            collective_id=0, has_side_effects=True, vmem_limit_bytes=60 * 1024 * 1024
        ),
        name="march",
    )(
        pressure_field,
        block_main.reshape(rows_here * 6, BS),
        block_coupled.reshape(rows_here * 6, BS),
        coupling.reshape(1, width),
        receivers.reshape(count // BS, BS),
        floors,
    )
    chips = lax.axis_size("freq") // 2
    span = NT // (2 * chips)
    total_freq = frequencies.shape[0]
    summed = pl.pallas_call(
        functools.partial(synth_kernel, chips, 1.0 / math.sqrt(total_freq)),
        out_shape=jax.ShapeDtypeStruct((span, half), F32),
        in_specs=[vmem, vmem],
        out_specs=vmem,
        scratch_shapes=[
            pltpu.VMEM((half, width), BF16),
            pltpu.VMEM((NT // 2, 2 * width), BF16),
            pltpu.VMEM((2, span, width), F32),
            pltpu.VMEM((2, chips, width), F32),
            pltpu.VMEM((chips, span, half), BF16),
            pltpu.VMEM((chips, span, half), BF16),
            dma,
            dma,
            dma((chips,)),
            dma((chips,)),
        ],
        compiler_params=pltpu.CompilerParams(collective_id=1, has_side_effects=True),
        name="synth",
    )(picked, frequencies.reshape(total_freq // BS, BS))
    return summed.T


def solution(mesh):
    in_specs = (
        P("depth", "freq"),
        P("depth", None, None, None),
        P("depth", None, None, None),
        P("freq"),
        P(),
        P(),
        P(),
    )
    out_specs = P("depth", "freq")
    return jax.shard_map(local, mesh=mesh, in_specs=in_specs, out_specs=out_specs, check_vma=False)
```

time: 532 us -> 78.6 us (0.15)
  the two profiles are of different devices: /device:TPU:1 before, /device:TPU:24 now
where the time goes in v1:
time: 78.6 us; the launch traced here: 78.4 us
  Pallas kernels  77 us (98%)
  local copies, waits for them, and re-layouts  1.38 us (2%)
    pallas_call x1, Pallas kernels, local(): pl.pallas_call(functools.partial(march_kernel, nb, unroll), out_shape=jax...  54.8 us
    pallas_call x1, Pallas kernels, local(): pl.pallas_call(functools.partial(synth_kernel, chips, 1.0 / math.sqrt(tot...  22.2 us

profile of v1, /device:TPU:24, one launch (start us, length us, event | category | flops | bytes accessed | tf_op | source)
XLA Modules:
  0.0 78.4 jit_solution(18441199637822788984)
XLA Ops:
  0.0 54.8 %march.1.picked = bf16[256,256]{1,0:T(8,128)(2,1)} custom-call(bf16[4096,256]{1,0:T(8,128)(2,1)} %field_hbm.1, bf16[24576,128]{1,0:T(8,128)(2,1)} %bitcast.6, bf16[24576,128]{1,0:T(8,128)(2,1)} %bitcast.7, f32[1,256]{1,0:T(1,128)} %bitcast.11, s32[4,128]{1,0:T(4,128)} %bitcast.10, s32[4]{0:T(128)} %floors.1), custom_call_target="tpu_custom_call" | custom-call | tf_op jit(solution)/shard_map/march/pallas_call | solution.py:437
  54.8 22.2 %synth.1 = f32[32,256]{1,0:T(8,128)} custom-call(bf16[256,256]{1,0:T(8,128)(2,1)} %march.1.picked, f32[64,128]{1,0:T(8,128)} %bitcast.9), custom_call_target="tpu_custom_call" | custom-call | tf_op jit(solution)/shard_map/synth/pallas_call | solution.py:480
  77.0 1.4 %copy.9 = f32[256,32]{0,1:T(8,128)} copy(f32[256,32]{0,1:T(8,128)} %bitcast.8) | data formatting | bytes 65536

commit v2 on v1

--- a/solution.py
+++ b/solution.py
@@ -46,7 +46,8 @@
     raw_main,
     raw_side,
     ops,
-    state,
+    state_a,
+    state_b,
     final,
     selector,
     recv_col,
@@ -67,41 +68,38 @@
     depth = lax.axis_index("depth")
     other = 1 - depth
     width = 2 * BS
-    rows_here = nb * BS
-    first_row = depth * rows_here
+    first_row = depth * nb * BS
     half = theirs.shape[0]
+    trips = nb // unroll
 
     def block_at(i):
         return jnp.where(depth == 0, i, nb - 1 - i)
 
-    edge = block_at(nb - 1)
-    halo_slot = jnp.where(depth == 0, nb + 1, 0)
-
-    def field_copy(b):
+    def rows_of(i, count):
+        return pl.ds(pl.multiple_of(i * count, count), count)
+
+    def field_copy(i):
         return pltpu.make_async_copy(
-            field_hbm.at[pl.ds(pl.multiple_of(b * BS, BS), BS), :],
-            raw_field.at[pl.ds(pl.multiple_of(b * BS, BS), BS), :],
-            field_sem.at[b],
-        )
-
-    def op_copy(hbm, raw, sem, b):
-        rows = 6 * BS
+            field_hbm.at[rows_of(block_at(i), BS), :],
+            raw_field.at[rows_of(i, BS), :],
+            field_sem.at[i],
+        )
+
+    def op_copy(hbm, raw, sem, i):
         return pltpu.make_async_copy(
-            hbm.at[pl.ds(pl.multiple_of(b * rows, rows), rows), :],
-            raw.at[pl.ds(pl.multiple_of(b * rows, rows), rows), :],
-            sem.at[b],
-        )
-
-    field_copy(edge).start()
+            hbm.at[rows_of(block_at(i), 6 * BS), :], raw.at[rows_of(i, 6 * BS), :], sem.at[i]
+        )
+
+    field_copy(nb - 1).start()
 
     @pl.loop(0, nb - 1)
     def _(i):
-        field_copy(block_at(i)).start()
+        field_copy(i).start()
 
     @pl.loop(0, nb)
     def _(i):
-        op_copy(main_hbm, raw_main, main_sem, block_at(i)).start()
-        op_copy(side_hbm, raw_side, side_sem, block_at(i)).start()
+        op_copy(main_hbm, raw_main, main_sem, i).start()
+        op_copy(side_hbm, raw_side, side_sem, i).start()
 
     barrier = pltpu.get_barrier_semaphore()
     pl.semaphore_signal(barrier, inc=1, device_id={"depth": other}, device_id_type=MESH)
@@ -110,11 +108,12 @@
     wanted = jnp.where(col < BS, 2 * col, 2 * (col - BS) + 1)
     split[...] = jnp.where(row == wanted, 1.0, 0.0).astype(BF16)
     row, col = iota((192, 192), 0), iota((192, 192), 1)
-    order[...] = jnp.where(col == 6 * (row & 31) + (row >> 5), 1.0, 0.0).astype(BF16)
-    split_f32 = split[...].astype(F32)
+    k, c, d = row >> 6, (row >> 5) & 1, row & 31
+    k = jnp.where(depth == 0, k, 2 - k)
+    order[...] = jnp.where(col == 6 * d + 2 * k + c, 1.0, 0.0).astype(BF16)
     weights[...] = jnp.dot(
         jnp.broadcast_to(coupling[...], (8, width)),
-        split_f32,
+        split[...].astype(F32),
         precision=lax.Precision.HIGHEST,
         preferred_element_type=F32,
     )
@@ -123,14 +122,12 @@
         tile = jnp.broadcast_to(spots[g : g + 1, :], (BS, BS))
         recv_col[g * BS : (g + 1) * BS, :] = tile.T
     empty = jnp.zeros((2 * BS, width), BF16)
-    for par in range(2):
-        state[par, 0 : 2 * BS, :] = empty
-        state[par, (nb + 1) * 2 * BS : (nb + 2) * 2 * BS, :] = empty
-
-    def put(par, slot, x):
-        start = pl.multiple_of(slot * 2 * BS, 2 * BS)
-        state[par, pl.ds(start, BS), :] = x
-        state[par, pl.ds(start + BS, BS), :] = times_unit(x)
+    for state in (state_a, state_b):
+        state[0 : 2 * BS, :] = empty
+
+    def put(state, slot, x):
+        state[rows_of(2 * slot, BS), :] = x
+        state[rows_of(2 * slot + 1, BS), :] = times_unit(x)
 
     def halo_copy(step, src):
         return pltpu.make_async_remote_copy(
@@ -142,119 +139,103 @@
             device_id_type=MESH,
         )
 
-    field_copy(edge).wait()
+    field_copy(nb - 1).wait()
     pl.semaphore_wait(barrier, 1)
-    edge_rows = pl.ds(pl.multiple_of(edge * BS, BS), BS)
-    first_halo = halo_copy(0, raw_field.at[edge_rows, :])
+    first_halo = halo_copy(0, raw_field.at[rows_of(nb - 1, BS), :])
     first_halo.start()
 
-    def deinterleave(b):
-        rows = pl.ds(pl.multiple_of(b * BS, BS), BS)
-        put(0, b + 1, dot(raw_field[rows, :], split[...]).astype(BF16))
-
-    @pl.loop(0, (nb - unroll) // unroll)
+    def deinterleave(i):
+        put(state_a, i + 1, dot(raw_field[rows_of(i, BS), :], split[...]).astype(BF16))
+
+    @pl.loop(0, nb - 1)
+    def _(i):
+        field_copy(i).wait()
+
+    @pl.loop(0, trips)
     def _(t):
         for u in range(unroll):
-            field_copy(block_at(t * unroll + u)).wait()
-        for u in range(unroll):
-            deinterleave(block_at(t * unroll + u))
-
-    for u in range(unroll - 1):
-        field_copy(block_at(nb - unroll + u)).wait()
-    for u in range(unroll):
-        deinterleave(block_at(nb - unroll + u))
-
-    def bring_in(b):
-        base = pl.multiple_of(b * 6 * BS, 6 * BS)
-        dest = pl.multiple_of(b * 2 * BS, 2 * BS)
+            deinterleave(t * unroll + u)
+
+    def bring_in(i):
         for q in range(4):
-            part = pl.ds(base + 192 * q, 192)
+            part = pl.ds(pl.multiple_of(i * 6 * BS, 6 * BS) + 192 * q, 192)
             both = jnp.concatenate([raw_main[part, :], raw_side[part, :]], axis=1)
             sorted_rows = dot(order[...], both).astype(BF16)
+            dest = pl.multiple_of(i * 2 * BS, 2 * BS) + 32 * q
             for kc in range(6):
                 tile = sorted_rows[32 * kc : 32 * kc + 32, :]
                 lanes = slice(kc * BS, (kc + 1) * BS)
-                ops[pl.ds(dest + 32 * q, 32), lanes] = tile[:, :BS]
-                ops[pl.ds(dest + BS + 32 * q, 32), lanes] = tile[:, BS:]
-
-    def select(b):
-        target = (first_row + b * BS).astype(F32)
+                ops[pl.ds(dest, 32), lanes] = tile[:, :BS]
+                ops[pl.ds(dest + BS, 32), lanes] = tile[:, BS:]
+
+    def select(i):
+        target = (first_row + block_at(i) * BS).astype(F32)
         lane = iota((2 * half, BS), 1).astype(F32) + target
-        lanes = pl.ds(pl.multiple_of(b * BS, BS), BS)
-        selector[:, lanes] = jnp.where(recv_col[...] == lane, 1.0, 0.0).astype(BF16)
-
-    def advance(step, par, b):
-        lhs = ops[pl.ds(pl.multiple_of(b * 2 * BS, 2 * BS), 2 * BS), :]
-        rhs = state[par, pl.ds(pl.multiple_of(b * 2 * BS, 2 * BS), 6 * BS), :]
-        product = dot(lhs, rhs)
+        selector[:, rows_of(i, BS)] = jnp.where(recv_col[...] == lane, 1.0, 0.0).astype(BF16)
+
+    def advance(step, state, i):
+        product = dot(ops[rows_of(i, 2 * BS), :], state[pl.ds(pl.multiple_of(i * 2 * BS, 2 * BS), 6 * BS), :])
         main, side = product[:BS], product[BS:]
         w_real, w_imag = weights[0:1, :BS], weights[0:1, BS:]
         side_real, side_imag = side[:, :BS], side[:, BS:]
         real = main[:, :BS] + (w_real * side_real - w_imag * side_imag)
         imag = main[:, BS:] + (w_real * side_imag + w_imag * side_real)
-        depth_index = first_row + b * BS + iota((BS, BS), 0)
+        depth_index = first_row + block_at(i) * BS + iota((BS, BS), 0)
         damping = jnp.where(depth_index >= floors[step], 0.5, 1.0).astype(F32)
         return jnp.concatenate([damping * real, damping * imag], axis=1).astype(BF16)
 
-    trips = nb // unroll
-
-    @pl.loop(0, trips)
+    def wait_ops(t):
+        for u in range(unroll):
+            op_copy(main_hbm, raw_main, main_sem, t * unroll + u).wait()
+            op_copy(side_hbm, raw_side, side_sem, t * unroll + u).wait()
+
+    wait_ops(0)
+    for u in range(unroll):
+        bring_in(u)
+        select(u)
+
+    @pl.loop(1, trips)
     def _(t):
-        @pl.when(t == trips - 1)
-        def _():
-            first_halo.wait()
-            put(0, halo_slot, dot(halo[0], split[...]).astype(BF16))
-
+        wait_ops(t)
         for u in range(unroll):
-            b = block_at(t * unroll + u)
-            op_copy(main_hbm, raw_main, main_sem, b).wait()
-            op_copy(side_hbm, raw_side, side_sem, b).wait()
-        for u in range(unroll):
-            b = block_at(t * unroll + u)
-            bring_in(b)
-            select(b)
-        for u in range(unroll):
-            b = block_at(t * unroll + u)
-            put(1, b + 1, advance(0, 0, b))
-
-    def edge_of(par):
-        return state.at[par, pl.ds(pl.multiple_of((edge + 1) * 2 * BS, 2 * BS), BS), :]
-
-    halo_copy(1, edge_of(1)).start()
-
-    @pl.loop(1, STEPS - 1)
-    def _(step):
-        par = step & 1
-
-        @pl.loop(0, trips)
-        def _(t):
-            @pl.when(t == trips - 1)
-            def _():
-                halo_copy(step, edge_of(par)).wait()
-                put(par, halo_slot, halo[step])
-
-            for u in range(unroll):
-                b = block_at(t * unroll + u)
-                put(1 - par, b + 1, advance(step, par, b))
-
-        halo_copy(step + 1, edge_of(1 - par)).start()
-
-    par = (STEPS - 1) & 1
-
-    @pl.loop(0, trips)
-    def _(t):
-        @pl.when(t == trips - 1)
-        def _():
-            halo_copy(STEPS - 1, edge_of(par)).wait()
-            put(par, halo_slot, halo[STEPS - 1])
-
-        for u in range(unroll):
-            b = block_at(t * unroll + u)
-            final[pl.ds(pl.multiple_of(b * BS, BS), BS), :] = advance(STEPS - 1, par, b)
+            put(state_b, (t - 1) * unroll + u + 1, advance(0, state_a, (t - 1) * unroll + u))
+            bring_in(t * unroll + u)
+            select(t * unroll + u)
+
+    first_halo.wait()
+    put(state_a, nb + 1, dot(halo[0], split[...]).astype(BF16))
+    for i in range(nb - unroll, nb):
+        put(state_b, i + 1, advance(0, state_a, i))
+
+    def edge_of(state):
+        return state.at[rows_of(2 * nb, BS), :]
+
+    states = (state_a, state_b)
+    for step in range(1, STEPS):
+        now, later = states[step % 2], states[1 - step % 2]
+        arrival = halo_copy(step, edge_of(now))
+        arrival.start()
+
+        def go(i):
+            x = advance(step, now, i)
+            if step < STEPS - 1:
+                put(later, i + 1, x)
+            else:
+                final[rows_of(i, BS), :] = x
+
+        for i in range(nb - unroll):
+            go(i)
+        arrival.wait()
+        put(now, nb + 1, halo[step])
+        for i in range(nb - unroll, nb):
+            go(i)
 
     def pick(owner):
-        rows = pl.ds(pl.multiple_of(owner * half, half), half)
-        return dot(selector[rows, :], final[...]).astype(BF16)
+        parts = []
+        for p in range(2):
+            rows = pl.ds(pl.multiple_of(owner * half, half) + p * (half // 2), half // 2)
+            parts.append(dot(selector[rows, :], final[...]).astype(BF16))
+        return jnp.concatenate(parts, axis=0)
 
     theirs[...] = pick(other)
     swap = pltpu.make_async_remote_copy(
@@ -444,7 +425,8 @@
             pltpu.VMEM((rows_here * 6, BS), BF16),
             pltpu.VMEM((rows_here * 6, BS), BF16),
             pltpu.VMEM((nb * 2 * BS, 6 * BS), BF16),
-            pltpu.VMEM((2, (nb + 2) * 2 * BS, width), BF16),
+            pltpu.VMEM(((nb + 2) * 2 * BS, width), BF16),
+            pltpu.VMEM(((nb + 2) * 2 * BS, width), BF16),
             pltpu.VMEM((rows_here, width), BF16),
             pltpu.VMEM((count, rows_here), BF16),
             pltpu.VMEM((count, BS), F32),

time: 78.6 us -> 58 us (0.74)
  Pallas kernels: 77 us -> 56.4 us
    pallas_call x1, Pallas kernels: 54.8 us -> 34.2 us  [local(): pl.pallas_call(functools.partial(march_kernel, nb, unroll), out_shape=jax...]
where the time goes in v2:
time: 58 us; the launch traced here: 57.8 us
  Pallas kernels  56.4 us (97%)
  local copies, waits for them, and re-layouts  1.38 us (2%)
    pallas_call x1, Pallas kernels, local(): pl.pallas_call(functools.partial(march_kernel, nb, unroll), out_shape=jax...  34.2 us
    pallas_call x1, Pallas kernels, local(): pl.pallas_call(functools.partial(synth_kernel, chips, 1.0 / math.sqrt(tot...  22.2 us
    unnamed x1, local copies, waits for them, and re-layouts  1.38 us

profile of v2, /device:TPU:24, one launch (start us, length us, event | category | flops | bytes accessed | tf_op | source)
XLA Modules:
  0.0 57.8 jit_solution(5287223964466481856)
XLA Ops:
  0.0 34.2 %march.1.picked = bf16[256,256]{1,0:T(8,128)(2,1)} custom-call(bf16[4096,256]{1,0:T(8,128)(2,1)} %field_hbm.1, bf16[24576,128]{1,0:T(8,128)(2,1)} %bitcast.6, bf16[24576,128]{1,0:T(8,128)(2,1)} %bitcast.7, f32[1,256]{1,0:T(1,128)} %bitcast.11, s32[4,128]{1,0:T(4,128)} %bitcast.10, s32[4]{0:T(128)} %floors.1), custom_call_target="tpu_custom_call" | custom-call | tf_op jit(solution)/shard_map/march/pallas_call | solution.py:418
  34.2 22.2 %synth.1 = f32[32,256]{1,0:T(8,128)} custom-call(bf16[256,256]{1,0:T(8,128)(2,1)} %march.1.picked, f32[64,128]{1,0:T(8,128)} %bitcast.9), custom_call_target="tpu_custom_call" | custom-call | tf_op jit(solution)/shard_map/synth/pallas_call | solution.py:462
  56.4 1.4 %copy.9 = f32[256,32]{0,1:T(8,128)} copy(f32[256,32]{0,1:T(8,128)} %bitcast.8) | data formatting | bytes 65536

commit v3 on v0

v3 whole, which is shorter than its diff:
```python
import functools
import math

import jax
import jax.numpy as jnp
from jax import lax
from jax.experimental import pallas as pl
from jax.experimental.pallas import tpu as pltpu
from jax.sharding import PartitionSpec as P

NT = 2048
STEPS = 4
BS = 128
MESH = pl.DeviceIdType.MESH
F32 = jnp.float32
BF16 = jnp.bfloat16


def iota(shape, dim):
    return lax.broadcasted_iota(jnp.int32, shape, dim)


def dot(a, b):
    return jnp.dot(a, b, preferred_element_type=F32)


def dot_nt(a, b):
    return lax.dot_general(a, b, (((1,), (1,)), ((), ())), preferred_element_type=F32)


def poly_coeffs():
    import numpy as np

    x = np.cos(np.pi * (np.arange(400) + 0.5) / 400) * 0.125 + 0.125
    y = np.sqrt(x)
    cheb_c = np.polynomial.chebyshev.Chebyshev.fit(x, np.cos(2 * np.pi * y), 8, domain=[0, 0.25])
    cheb_s = np.polynomial.chebyshev.Chebyshev.fit(x, np.sin(2 * np.pi * y) / y, 8, domain=[0, 0.25])
    to = np.polynomial.polynomial.Polynomial
    return (
        [float(v) for v in cheb_c.convert(kind=to).coef],
        [float(v) for v in cheb_s.convert(kind=to).coef],
    )


COS_COEFFS, SIN_COEFFS = poly_coeffs()


def horner(coeffs, z):
    total = jnp.full_like(z, coeffs[-1])
    for c in reversed(coeffs[:-1]):
        total = total * z + c
    return total


def cos_sin(turns):
    r = turns - jnp.floor(turns + 0.5)
    z = r * r
    return horner(COS_COEFFS, z), r * horner(SIN_COEFFS, z)


def torus_offsets(chips):
    if chips != 32:
        return None
    found = []
    for dx in range(4):
        for dy in range(4):
            for dh in range(2):
                if dx or dy or dh:
                    found.append((min(dx, 4 - dx) + min(dy, 4 - dy) + 2 * dh, dx, dy, dh))
    return [entry[1:] for entry in sorted(found, key=lambda entry: (-entry[0],) + entry[1:])]


def peers_of(chip, chips, sign):
    offsets = torus_offsets(chips)
    if offsets is None:
        return [(chip + sign * k + chips) % chips for k in range(1, chips)]
    x, y, h = chip // 8, (chip // 2) % 4, chip % 2
    return [
        (((x + sign * dx + 4) % 4) * 4 + (y + sign * dy + 4) % 4) * 2 + (h + dh) % 2
        for dx, dy, dh in offsets
    ]


def kernel(
    nb,
    unroll,
    chips,
    factor,
    field_hbm,
    main_hbm,
    side_hbm,
    coupling_hbm,
    frequencies_hbm,
    receivers_hbm,
    floors,
    out,
    raw_field,
    raw_main,
    raw_side,
    ops,
    state_a,
    state_b,
    final_real,
    final_imag,
    selector,
    recv_col,
    weights,
    split,
    order,
    first_halo,
    halo,
    theirs,
    arrived,
    own,
    mate,
    basis,
    near,
    far,
    sums,
    inbox,
    coupling,
    frequencies,
    receivers,
    field_sem,
    main_sem,
    side_sem,
    small_sem,
    halo_send,
    halo_recv,
    swap_send,
    swap_recv,
    pair_send,
    pair_recv,
    out_send,
    out_recv,
):
    depth, me = lax.axis_index("depth"), lax.axis_index("freq")
    other = 1 - depth
    chip, core = me // 2, me % 2
    mate_id = 2 * chip + (1 - core)
    width = 2 * BS
    first_row = depth * nb * BS
    half = 2 * BS
    trips = nb // unroll
    span = NT // (2 * chips)

    def block_at(i):
        return jnp.where(depth == 0, i, nb - 1 - i)

    def rows_of(i, count):
        return pl.ds(pl.multiple_of(i * count, count), count)

    def field_copy(i):
        return pltpu.make_async_copy(
            field_hbm.at[rows_of(block_at(i), BS), :],
            raw_field.at[rows_of(i, BS), :],
            field_sem.at[i],
        )

    def op_copy(hbm, raw, sem, i):
        return pltpu.make_async_copy(
            hbm.at[rows_of(block_at(i), 6 * BS), :], raw.at[rows_of(i, 6 * BS), :], sem.at[i]
        )

    small = [
        pltpu.make_async_copy(coupling_hbm, coupling, small_sem.at[0]),
        pltpu.make_async_copy(receivers_hbm, receivers, small_sem.at[1]),
        pltpu.make_async_copy(frequencies_hbm, frequencies, small_sem.at[2]),
    ]
    for copy in small:
        copy.start()
    field_copy(nb - 1).start()

    @pl.loop(0, nb - 1)
    def _(i):
        field_copy(i).start()

    @pl.loop(0, nb)
    def _(i):
        op_copy(main_hbm, raw_main, main_sem, i).start()
        op_copy(side_hbm, raw_side, side_sem, i).start()

    barrier = pltpu.get_barrier_semaphore()

    def greet(target):
        pl.semaphore_signal(barrier, inc=1, device_id=target, device_id_type=MESH)

    greet({"depth": other})
    greet({"freq": mate_id})

    @pl.loop(1, chips)
    def _(k):
        greet({"freq": 2 * ((chip + k) % chips) + core})

    row, col = iota((width, width), 0), iota((width, width), 1)
    wanted = jnp.where(col < BS, 2 * col, 2 * (col - BS) + 1)
    split[...] = jnp.where(row == wanted, 1.0, 0.0).astype(BF16)
    row, col = iota((192, 192), 0), iota((192, 192), 1)
    k, c, d = row >> 6, (row >> 5) & 1, row & 31
    k = jnp.where(depth == 0, k, 2 - k)
    order[...] = jnp.where(col == 6 * d + 2 * k + c, 1.0, 0.0).astype(BF16)
    empty = jnp.zeros((3 * BS, BS), BF16)
    state_a[0 : 3 * BS, :] = empty
    state_b[0 : 3 * BS, :] = empty
    for copy in small:
        copy.wait()
    weights[...] = jnp.dot(
        jnp.broadcast_to(coupling[...], (8, width)),
        split[...].astype(F32),
        precision=lax.Precision.HIGHEST,
        preferred_element_type=F32,
    )
    spots = receivers[...].astype(F32)
    for g in range(receivers.shape[0]):
        tile = jnp.broadcast_to(spots[g : g + 1, :], (BS, BS))
        recv_col[g * BS : (g + 1) * BS, :] = tile.T

    freq = jnp.concatenate([frequencies[pl.ds(me, 1), :], frequencies[pl.ds(mate_id, 1), :]], axis=1)
    scale = 1.0 / NT
    near_n = iota((span, width), 0).astype(F32)
    near[0], near[1] = cos_sin(freq * near_n * scale)
    far_n = ((2 * iota((chips, width), 0) + core) * span).astype(F32)
    far[0], far[1] = cos_sin(freq * far_n * scale)

    def make_basis(j):
        ca, sa = far[0, j : j + 1, :], far[1, j : j + 1, :]
        cb, sb = near[0], near[1]
        real = (ca * cb - sa * sb).astype(BF16)
        imag = (-(sa * cb + ca * sb)).astype(BF16)
        for q, part in enumerate((real[:, :BS], imag[:, :BS], real[:, BS:], imag[:, BS:])):
            basis[q, j * span : (j + 1) * span, :] = part

    def put(state, slot, real, imag):
        state[rows_of(3 * slot, BS), :] = real
        state[rows_of(3 * slot + 1, BS), :] = imag
        state[rows_of(3 * slot + 2, BS), :] = -imag

    def remote(src, dst, send, recv, target):
        return pltpu.make_async_remote_copy(
            src_ref=src,
            dst_ref=dst,
            send_sem=send,
            recv_sem=recv,
            device_id=target,
            device_id_type=MESH,
        )

    def put_raw(slot, block):
        x = dot(block, split[...]).astype(BF16)
        put(state_a, slot, x[:, :BS], x[:, BS:])

    @pl.loop(0, nb)
    def _(i):
        field_copy(i).wait()

    @pl.loop(0, trips)
    def _(t):
        for u in range(unroll):
            put_raw(t * unroll + u + 1, raw_field[rows_of(t * unroll + u, BS), :])

    def bring_in(i):
        for q in range(4):
            part = pl.ds(pl.multiple_of(i * 6 * BS, 6 * BS) + 192 * q, 192)
            both = jnp.concatenate([raw_main[part, :], raw_side[part, :]], axis=1)
            sorted_rows = dot(order[...], both).astype(BF16)
            for kc in range(6):
                tile = sorted_rows[32 * kc : 32 * kc + 32, :]
                dest = pl.multiple_of(i * 12 * BS, 12 * BS) + kc * 2 * BS + 32 * q
                ops[pl.ds(dest, 32), :] = tile[:, :BS]
                ops[pl.ds(dest + BS, 32), :] = tile[:, BS:]

    def select(i):
        target = (first_row + block_at(i) * BS).astype(F32)
        lane = iota((2 * half, BS), 1).astype(F32) + target
        selector[rows_of(i, 2 * half), :] = jnp.where(recv_col[...] == lane, 1.0, 0.0).astype(BF16)

    def advance(step, state, i):
        lhs = jnp.concatenate([ops[rows_of(6 * i + kc, 2 * BS), :] for kc in range(6)], axis=1)
        tiles = []
        for slot in (i, i + 1, i + 2):
            real, imag, minus = (state[rows_of(3 * slot + q, BS), :] for q in range(3))
            tiles.append(jnp.concatenate([real, imag], axis=1))
            tiles.append(jnp.concatenate([minus, real], axis=1))
        product = dot(lhs, jnp.concatenate(tiles, axis=0))
        main, side = product[:BS], product[BS:]
        w_real, w_imag = weights[0:1, :BS], weights[0:1, BS:]
        side_real, side_imag = side[:, :BS], side[:, BS:]
        real = main[:, :BS] + (w_real * side_real - w_imag * side_imag)
        imag = main[:, BS:] + (w_real * side_imag + w_imag * side_real)
        depth_index = first_row + block_at(i) * BS + iota((BS, BS), 0)
        damping = jnp.where(depth_index >= floors[step], 0.5, 1.0).astype(F32)
        return (damping * real).astype(BF16), (damping * imag).astype(BF16)

    def load_group(t):
        for u in range(unroll):
            op_copy(main_hbm, raw_main, main_sem, t * unroll + u).wait()
            op_copy(side_hbm, raw_side, side_sem, t * unroll + u).wait()

    def first_step(i):
        put(state_b, i + 1, *advance(0, state_a, i))

    def pipelined(t):
        load_group(t)
        for u in range(unroll):
            first_step((t - 1) * unroll + u)
            bring_in(t * unroll + u)
            select(t * unroll + u)

    load_group(0)
    for u in range(unroll):
        bring_in(u)
        select(u)
    pipelined(1)
    pl.semaphore_wait(barrier, chips + 1)
    start_halo = remote(
        raw_field.at[rows_of(nb - 1, BS), :],
        first_halo,
        halo_send.at[0],
        halo_recv.at[0],
        {"depth": other},
    )
    start_halo.start()
    pl.loop(2, trips)(pipelined)
    start_halo.wait()
    put_raw(nb + 1, first_halo[...])
    for i in range(nb - unroll, nb):
        first_step(i)

    states = (state_a, state_b)
    for step in range(1, STEPS):
        now, later = states[step % 2], states[1 - step % 2]
        arrival = remote(
            now.at[pl.ds(3 * nb * BS, 2 * BS), :],
            halo.at[step],
            halo_send.at[step],
            halo_recv.at[step],
            {"depth": other},
        )
        arrival.start()
        for i in range(nb):
            if i == nb - unroll:
                arrival.wait()
                put(now, nb + 1, halo[step, :BS, :], halo[step, BS:, :])
            real, imag = advance(step, now, i)
            if step < STEPS - 1:
                put(later, i + 1, real, imag)
            else:
                final_real[rows_of(i, BS), :] = real
                final_imag[rows_of(i, BS), :] = imag
            if step == 1:
                for j in range(i * chips // nb, (i + 1) * chips // nb):
                    make_basis(j)

    def pick(owner, p):
        rows = owner * half + p * BS
        lhs = jnp.concatenate(
            [selector[pl.ds(pl.multiple_of(rows + i * 2 * half, BS), BS), :] for i in range(nb)], axis=1
        )
        rhs = jnp.concatenate([final_real[...], final_imag[...]], axis=1)
        x = dot(lhs, rhs).astype(BF16)
        return x[:, :BS], x[:, BS:]

    def swap(p):
        return remote(
            theirs.at[p], arrived.at[p], swap_send.at[p], swap_recv.at[p], {"depth": other}
        )

    def pair(p):
        return remote(own.at[p], mate.at[p], pair_send.at[p], pair_recv.at[p], {"freq": mate_id})

    for p in range(2):
        theirs[p, :BS, :], theirs[p, BS:, :] = pick(other, p)
    for p in range(2):
        swap(p).start()
    mine = [pick(depth, p) for p in range(2)]
    for p in range(2):
        swap(p).wait_recv()
        own[p, :BS, :] = mine[p][0] + arrived[p, :BS, :]
        own[p, BS:, :] = mine[p][1] + arrived[p, BS:, :]
        pair(p).start()

    targets = peers_of(chip, chips, 1)

    def outgoing(p, k):
        return remote(
            sums.at[p, targets[k]],
            inbox.at[p, k],
            out_send.at[p, k],
            out_recv.at[p, k],
            {"freq": 2 * targets[k] + core},
        )

    for p in range(2):
        pair(p).wait_recv()
        rhs = jnp.concatenate([own[p, :BS, :], own[p, BS:, :], mate[p, :BS, :], mate[p, BS:, :]], axis=1)
        group = min(8, chips)
        for g in range(chips // group):
            place = slice(g * group * span, (g + 1) * group * span)
            lhs = jnp.concatenate([basis[q, place, :] for q in range(4)], axis=1)
            part = (dot_nt(lhs, rhs) * factor).astype(BF16)
            for u in range(group):
                sums[p, g * group + u] = part[u * span : (u + 1) * span, :]
        for k in range(chips - 1):
            outgoing(p, k).start()

    for p in range(2):
        total = sums[p, chip].astype(F32)
        for k in range(chips - 1):
            outgoing(p, k).wait_recv()
        for k in range(chips - 1):
            total = total + inbox[p, k].astype(F32)
        out[:, p * BS : (p + 1) * BS] = total

    for p in range(2):
        swap(p).wait_send()
        pair(p).wait_send()
        for k in range(chips - 1):
            outgoing(p, k).wait_send()


def local(pressure_field, block_main, block_coupled, coupling, frequencies, receivers, floors):
    rows_here, width = pressure_field.shape
    nb = rows_here // BS
    unroll = min(8, nb // 2)
    count = receivers.shape[0]
    half = count // 2
    total_freq = frequencies.shape[0]
    chips = lax.axis_size("freq") // 2
    span = NT // (2 * chips)
    any_space = pl.BlockSpec(memory_space=pl.ANY)
    vmem = pl.BlockSpec(memory_space=pltpu.VMEM)
    smem = pl.BlockSpec(memory_space=pltpu.SMEM)
    dma = pltpu.SemaphoreType.DMA
    summed = pl.pallas_call(
        functools.partial(kernel, nb, unroll, chips, 1.0 / math.sqrt(total_freq)),
        out_shape=jax.ShapeDtypeStruct((span, half), F32),
        in_specs=[any_space] * 6 + [smem],
        out_specs=vmem,
        scratch_shapes=[
            pltpu.VMEM((rows_here, width), BF16),
            pltpu.VMEM((rows_here * 6, BS), BF16),
            pltpu.VMEM((rows_here * 6, BS), BF16),
            pltpu.VMEM((nb * 12 * BS, BS), BF16),
            pltpu.VMEM(((nb + 2) * 3 * BS, BS), BF16),
            pltpu.VMEM(((nb + 2) * 3 * BS, BS), BF16),
            pltpu.VMEM((rows_here, BS), BF16),
            pltpu.VMEM((rows_here, BS), BF16),
            pltpu.VMEM((nb * count, BS), BF16),
            pltpu.VMEM((count, BS), F32),
            pltpu.VMEM((8, width), F32),
            pltpu.VMEM((width, width), BF16),
            pltpu.VMEM((192, 192), BF16),
            pltpu.VMEM((BS, width), BF16),
            pltpu.VMEM((STEPS, 2 * BS, BS), BF16),
            pltpu.VMEM((2, 2 * BS, BS), BF16),
            pltpu.VMEM((2, 2 * BS, BS), BF16),
            pltpu.VMEM((2, 2 * BS, BS), BF16),
            pltpu.VMEM((2, 2 * BS, BS), BF16),
            pltpu.VMEM((4, NT // 2, BS), BF16),
            pltpu.VMEM((2, span, width), F32),
            pltpu.VMEM((2, chips, width), F32),
            pltpu.VMEM((2, chips, span, BS), BF16),
            pltpu.VMEM((2, chips, span, BS), BF16),
            pltpu.VMEM((1, width), F32),
            pltpu.VMEM((total_freq // BS, BS), F32),
            pltpu.VMEM((count // BS, BS), jnp.int32),
            dma((nb,)),
            dma((nb,)),
            dma((nb,)),
            dma((3,)),
            dma((STEPS,)),
            dma((STEPS,)),
            dma((2,)),
            dma((2,)),
            dma((2,)),
            dma((2,)),
            dma((2, chips)),
            dma((2, chips)),
        ],
        compiler_params=pltpu.CompilerParams(
            collective_id=0, has_side_effects=True, vmem_limit_bytes=60 * 1024 * 1024
        ),
        name="march",
    )(
        pressure_field,
        block_main.reshape(rows_here * 6, BS),
        block_coupled.reshape(rows_here * 6, BS),
        coupling.reshape(1, width),
        frequencies.reshape(total_freq // BS, BS),
        receivers.reshape(count // BS, BS),
        floors,
    )
    return summed.T


def solution(mesh):
    in_specs = (
        P("depth", "freq"),
        P("depth", None, None, None),
        P("depth", None, None, None),
        P("freq"),
        P(),
        P(),
        P(),
    )
    out_specs = P("depth", "freq")
    return jax.shard_map(local, mesh=mesh, in_specs=in_specs, out_specs=out_specs, check_vma=False)
```

time: 532 us -> 50.1 us (0.09)
  local copies, waits for them, and re-layouts: 170 us -> 1.38 us
  matrix products: 160 us -> 0 us
  other arithmetic: 122 us -> 0 us
  Pallas kernels: 0 us -> 48.6 us
  blocking collectives: 45.7 us -> 0 us
  starting transfers between devices: 25.8 us -> 0 us
    dot_general x26 -> x0, matrix products: 160 us -> none  [the longest x24 156 us: apply_blocks(): jnp.einsum('bij,bjc->bic', ordered[:, offset], stacked[offset:offset + bl...]
    slice x37 -> x0, local copies, waits for them, and re-layouts: 124 us -> none  [the longest x24 74.9 us: times_unit(): lower = jnp.roll(values, 1, axis=1)]
    convert_element_type x7 -> x0, other arithmetic: 88.7 us -> none  [local(): columns = (damping[:, None] * combined).astype(jnp.bfloat16)]
    pallas_call x0 -> x1, Pallas kernels: none -> 48.6 us  [local(): pl.pallas_call(functools.partial(kernel, nb, unroll, chips, 1.0 / math.sq...]
    all_to_all x1 -> x0, blocking collectives: 45.7 us -> none  [summed_on_arrival_2(): lax.all_to_all(parts, axis, split_axis=0, concat_axis=0, tiled=True)]
    unnamed x128 -> x1, local copies, waits for them, and re-layouts: 25.3 us -> 1.38 us
    ppermute x8 -> x0, starting transfers between devices: 22.1 us -> none  [the longest x4 16.3 us: padded_2(): lax.ppermute(tail, axis, [(i, (i + 1) % count) for i in range(ends)])]
    add x4 -> x0, other arithmetic: 14.6 us -> none  [apply_blocks(): return real_part + times_unit(imag_part)]
  transfers between devices with their start and end apart: 9 -> 0, of which waited for: 2 -> 0; matrix products, arithmetic and copies ran while one was open for 11% -> 0% of each run, Pallas kernels for 0% -> 0%
where the time goes in v3:
time: 50.1 us; the launch traced here: 49.9 us
  Pallas kernels  48.6 us (97%)
  local copies, waits for them, and re-layouts  1.38 us (3%)
    pallas_call x1, Pallas kernels, local(): pl.pallas_call(functools.partial(kernel, nb, unroll, chips, 1.0 / math.sq...  48.6 us
    unnamed x1, local copies, waits for them, and re-layouts  1.38 us

profile of v3, /device:TPU:1, one launch (start us, length us, event | category | flops | bytes accessed | tf_op | source)
XLA Modules:
  0.0 49.9 jit_solution(11912748332757886670)
XLA Ops:
  0.0 48.6 %march.1 = f32[32,256]{1,0:T(8,128)} custom-call(bf16[4096,256]{1,0:T(8,128)(2,1)} %field_hbm.1, bf16[24576,128]{1,0:T(8,128)(2,1)} %bitcast.6, bf16[24576,128]{1,0:T(8,128)(2,1)} %bitcast.7, f32[1,256]{1,0:T(1,128)} %bitcast.11, f32[64,128]{1,0:T(8,128)} %bitcast.9, s32[4,128]{1,0:T(4,128)} %bitcast.10, s32[4]{0:T(128)} %floors.1), custom_call_target="tpu_custom_call" | custom-call | tf_op jit(solution)/shard_map/march/pallas_call | solution.py:434
  48.6 1.4 %copy.9 = f32[256,32]{0,1:T(8,128)} copy(f32[256,32]{0,1:T(8,128)} %bitcast.8) | data formatting | bytes 65536

commit v4 on v3

--- a/solution.py
+++ b/solution.py
@@ -83,7 +83,6 @@
 
 def kernel(
     nb,
-    unroll,
     chips,
     factor,
     field_hbm,
@@ -141,7 +140,6 @@
     width = 2 * BS
     first_row = depth * nb * BS
     half = 2 * BS
-    trips = nb // unroll
     span = NT // (2 * chips)
 
     def block_at(i):
@@ -253,10 +251,8 @@
     def _(i):
         field_copy(i).wait()
 
-    @pl.loop(0, trips)
-    def _(t):
-        for u in range(unroll):
-            put_raw(t * unroll + u + 1, raw_field[rows_of(t * unroll + u, BS), :])
+    for i in range(nb):
+        put_raw(i + 1, raw_field[rows_of(i, BS), :])
 
     def bring_in(i):
         for q in range(4):
@@ -291,55 +287,57 @@
         damping = jnp.where(depth_index >= floors[step], 0.5, 1.0).astype(F32)
         return (damping * real).astype(BF16), (damping * imag).astype(BF16)
 
-    def load_group(t):
-        for u in range(unroll):
-            op_copy(main_hbm, raw_main, main_sem, t * unroll + u).wait()
-            op_copy(side_hbm, raw_side, side_sem, t * unroll + u).wait()
+    def load_group(first, last):
+        for i in range(first, last):
+            op_copy(main_hbm, raw_main, main_sem, i).wait()
+            op_copy(side_hbm, raw_side, side_sem, i).wait()
 
     def first_step(i):
         put(state_b, i + 1, *advance(0, state_a, i))
 
-    def pipelined(t):
-        load_group(t)
-        for u in range(unroll):
-            first_step((t - 1) * unroll + u)
-            bring_in(t * unroll + u)
-            select(t * unroll + u)
-
-    load_group(0)
-    for u in range(unroll):
-        bring_in(u)
-        select(u)
-    pipelined(1)
-    pl.semaphore_wait(barrier, chips + 1)
-    start_halo = remote(
-        raw_field.at[rows_of(nb - 1, BS), :],
-        first_halo,
-        halo_send.at[0],
-        halo_recv.at[0],
-        {"depth": other},
-    )
-    start_halo.start()
-    pl.loop(2, trips)(pipelined)
-    start_halo.wait()
+    states = (state_a, state_b)
+
+    def arrival(step):
+        if step == 0:
+            source, target = raw_field.at[rows_of(nb - 1, BS), :], first_halo
+        else:
+            source, target = states[step % 2].at[pl.ds(3 * nb * BS, 2 * BS), :], halo.at[step]
+        return remote(source, target, halo_send.at[step], halo_recv.at[step], {"depth": other})
+
+    bounds = [0, max(1, 3 * nb // 16), nb // 2, nb]
+    load_group(0, bounds[1])
+    for i in range(bounds[1]):
+        bring_in(i)
+        select(i)
+    for g in (1, 2):
+        load_group(bounds[g], bounds[g + 1])
+        if g == 2:
+            pl.semaphore_wait(barrier, chips + 1)
+            arrival(0).start()
+        ready, coming = bounds[g] - bounds[g - 1], bounds[g + 1] - bounds[g]
+        done = 0
+        for n in range(coming):
+            bring_in(bounds[g] + n)
+            select(bounds[g] + n)
+            while done * coming < (n + 1) * ready:
+                first_step(bounds[g - 1] + done)
+                done += 1
+    middle = bounds[2] + (nb - bounds[2]) // 2
+    for i in range(bounds[2], middle):
+        first_step(i)
+    arrival(0).wait()
     put_raw(nb + 1, first_halo[...])
-    for i in range(nb - unroll, nb):
+    first_step(nb - 1)
+    arrival(1).start()
+    for i in range(middle, nb - 1):
         first_step(i)
 
-    states = (state_a, state_b)
     for step in range(1, STEPS):
         now, later = states[step % 2], states[1 - step % 2]
-        arrival = remote(
-            now.at[pl.ds(3 * nb * BS, 2 * BS), :],
-            halo.at[step],
-            halo_send.at[step],
-            halo_recv.at[step],
-            {"depth": other},
-        )
-        arrival.start()
-        for i in range(nb):
-            if i == nb - unroll:
-                arrival.wait()
+        turn = nb - 1 if step == STEPS - 1 else nb - max(1, nb // (8 * step))
+        for i in list(range(turn)) + [nb - 1] + list(range(turn, nb - 1)):
+            if i == nb - 1:
+                arrival(step).wait()
                 put(now, nb + 1, halo[step, :BS, :], halo[step, BS:, :])
             real, imag = advance(step, now, i)
             if step < STEPS - 1:
@@ -347,6 +345,8 @@
             else:
                 final_real[rows_of(i, BS), :] = real
                 final_imag[rows_of(i, BS), :] = imag
+            if i == nb - 1 and step < STEPS - 1:
+                arrival(step + 1).start()
             if step == 1:
                 for j in range(i * chips // nb, (i + 1) * chips // nb):
                     make_basis(j)
@@ -421,7 +421,6 @@
 def local(pressure_field, block_main, block_coupled, coupling, frequencies, receivers, floors):
     rows_here, width = pressure_field.shape
     nb = rows_here // BS
-    unroll = min(8, nb // 2)
     count = receivers.shape[0]
     half = count // 2
     total_freq = frequencies.shape[0]
@@ -432,7 +431,7 @@
     smem = pl.BlockSpec(memory_space=pltpu.SMEM)
     dma = pltpu.SemaphoreType.DMA
     summed = pl.pallas_call(
-        functools.partial(kernel, nb, unroll, chips, 1.0 / math.sqrt(total_freq)),
+        functools.partial(kernel, nb, chips, 1.0 / math.sqrt(total_freq)),
         out_shape=jax.ShapeDtypeStruct((span, half), F32),
         in_specs=[any_space] * 6 + [smem],
         out_specs=vmem,

time: 50.1 us -> 48.9 us (0.976)
  Pallas kernels: 48.6 us -> 47.4 us
    pallas_call x1, Pallas kernels: 48.6 us -> 47.4 us  [local(): pl.pallas_call(functools.partial(kernel, nb, chips, 1.0 / math.sqrt(total...]
where the time goes in v4:
time: 48.9 us; the launch traced here: 48.8 us
  Pallas kernels  47.4 us (97%)
  local copies, waits for them, and re-layouts  1.38 us (3%)
    pallas_call x1, Pallas kernels, local(): pl.pallas_call(functools.partial(kernel, nb, chips, 1.0 / math.sqrt(total...  47.4 us
    unnamed x1, local copies, waits for them, and re-layouts  1.38 us

profile of v4, /device:TPU:1, one launch (start us, length us, event | category | flops | bytes accessed | tf_op | source)
XLA Modules:
  0.0 48.8 jit_solution(6327514889942192964)
XLA Ops:
  0.0 47.4 %march.1 = f32[32,256]{1,0:T(8,128)} custom-call(bf16[4096,256]{1,0:T(8,128)(2,1)} %field_hbm.1, bf16[24576,128]{1,0:T(8,128)(2,1)} %bitcast.6, bf16[24576,128]{1,0:T(8,128)(2,1)} %bitcast.7, f32[1,256]{1,0:T(1,128)} %bitcast.11, f32[64,128]{1,0:T(8,128)} %bitcast.9, s32[4,128]{1,0:T(4,128)} %bitcast.10, s32[4]{0:T(128)} %floors.1), custom_call_target="tpu_custom_call" | custom-call | tf_op jit(solution)/shard_map/march/pallas_call | solution.py:433
  47.4 1.4 %copy.9 = f32[256,32]{0,1:T(8,128)} copy(f32[256,32]{0,1:T(8,128)} %bitcast.8) | data formatting | bytes 65536

commit v5 on v4

--- a/solution.py
+++ b/solution.py
@@ -91,7 +91,7 @@
     coupling_hbm,
     frequencies_hbm,
     receivers_hbm,
-    floors,
+    floors_hbm,
     out,
     raw_field,
     raw_main,
@@ -120,6 +120,7 @@
     coupling,
     frequencies,
     receivers,
+    floors,
     field_sem,
     main_sem,
     side_sem,
@@ -152,31 +153,37 @@
         return pltpu.make_async_copy(
             field_hbm.at[rows_of(block_at(i), BS), :],
             raw_field.at[rows_of(i, BS), :],
-            field_sem.at[i],
+            field_sem,
         )
+
+    bounds = [0, max(1, 3 * nb // 16), nb // 2, nb]
 
     def op_copy(hbm, raw, sem, i):
         return pltpu.make_async_copy(
-            hbm.at[rows_of(block_at(i), 6 * BS), :], raw.at[rows_of(i, 6 * BS), :], sem.at[i]
+            hbm.at[rows_of(block_at(i), 6 * BS), :], raw.at[rows_of(i, 6 * BS), :], sem
         )
+
+    def wait_local(place, sem):
+        pltpu.make_async_copy(place, place, sem).wait()
 
     small = [
         pltpu.make_async_copy(coupling_hbm, coupling, small_sem.at[0]),
         pltpu.make_async_copy(receivers_hbm, receivers, small_sem.at[1]),
         pltpu.make_async_copy(frequencies_hbm, frequencies, small_sem.at[2]),
+        pltpu.make_async_copy(floors_hbm, floors, small_sem.at[3]),
     ]
     for copy in small:
         copy.start()
-    field_copy(nb - 1).start()
-
-    @pl.loop(0, nb - 1)
+    @pl.loop(0, nb)
     def _(i):
         field_copy(i).start()
 
-    @pl.loop(0, nb)
-    def _(i):
-        op_copy(main_hbm, raw_main, main_sem, i).start()
-        op_copy(side_hbm, raw_side, side_sem, i).start()
+    for g in range(3):
+
+        @pl.loop(bounds[g], bounds[g + 1])
+        def _(i):
+            op_copy(main_hbm, raw_main, main_sem.at[g], i).start()
+            op_copy(side_hbm, raw_side, side_sem.at[g], i).start()
 
     barrier = pltpu.get_barrier_semaphore()
 
@@ -247,13 +254,6 @@
         x = dot(block, split[...]).astype(BF16)
         put(state_a, slot, x[:, :BS], x[:, BS:])
 
-    @pl.loop(0, nb)
-    def _(i):
-        field_copy(i).wait()
-
-    for i in range(nb):
-        put_raw(i + 1, raw_field[rows_of(i, BS), :])
-
     def bring_in(i):
         for q in range(4):
             part = pl.ds(pl.multiple_of(i * 6 * BS, 6 * BS) + 192 * q, 192)
@@ -287,10 +287,10 @@
         damping = jnp.where(depth_index >= floors[step], 0.5, 1.0).astype(F32)
         return (damping * real).astype(BF16), (damping * imag).astype(BF16)
 
-    def load_group(first, last):
-        for i in range(first, last):
-            op_copy(main_hbm, raw_main, main_sem, i).wait()
-            op_copy(side_hbm, raw_side, side_sem, i).wait()
+    def load_group(g):
+        rows = pl.ds(bounds[g] * 6 * BS, (bounds[g + 1] - bounds[g]) * 6 * BS)
+        wait_local(raw_main.at[rows, :], main_sem.at[g])
+        wait_local(raw_side.at[rows, :], side_sem.at[g])
 
     def first_step(i):
         put(state_b, i + 1, *advance(0, state_a, i))
@@ -304,13 +304,15 @@
             source, target = states[step % 2].at[pl.ds(3 * nb * BS, 2 * BS), :], halo.at[step]
         return remote(source, target, halo_send.at[step], halo_recv.at[step], {"depth": other})
 
-    bounds = [0, max(1, 3 * nb // 16), nb // 2, nb]
-    load_group(0, bounds[1])
+    wait_local(raw_field, field_sem)
+    load_group(0)
+    for i in range(nb):
+        put_raw(i + 1, raw_field[rows_of(i, BS), :])
     for i in range(bounds[1]):
         bring_in(i)
         select(i)
     for g in (1, 2):
-        load_group(bounds[g], bounds[g + 1])
+        load_group(g)
         if g == 2:
             pl.semaphore_wait(barrier, chips + 1)
             arrival(0).start()
@@ -327,14 +329,16 @@
         first_step(i)
     arrival(0).wait()
     put_raw(nb + 1, first_halo[...])
-    first_step(nb - 1)
+    between = max(1, nb // 10)
+    for i in [nb - 1] + list(range(middle, middle + between)):
+        first_step(i)
     arrival(1).start()
-    for i in range(middle, nb - 1):
+    for i in range(middle + between, nb - 1):
         first_step(i)
 
     for step in range(1, STEPS):
         now, later = states[step % 2], states[1 - step % 2]
-        turn = nb - 1 if step == STEPS - 1 else nb - max(1, nb // (8 * step))
+        turn = nb - 1 if step == STEPS - 1 else nb - 1 - between - (2 - step) * between
         for i in list(range(turn)) + [nb - 1] + list(range(turn, nb - 1)):
             if i == nb - 1:
                 arrival(step).wait()
@@ -345,7 +349,7 @@
             else:
                 final_real[rows_of(i, BS), :] = real
                 final_imag[rows_of(i, BS), :] = imag
-            if i == nb - 1 and step < STEPS - 1:
+            if i == turn + between - 1 and step < STEPS - 1:
                 arrival(step + 1).start()
             if step == 1:
                 for j in range(i * chips // nb, (i + 1) * chips // nb):
@@ -385,8 +389,8 @@
         return remote(
             sums.at[p, targets[k]],
             inbox.at[p, k],
-            out_send.at[p, k],
-            out_recv.at[p, k],
+            out_send.at[p],
+            out_recv.at[p],
             {"freq": 2 * targets[k] + core},
         )
 
@@ -405,8 +409,7 @@
 
     for p in range(2):
         total = sums[p, chip].astype(F32)
-        for k in range(chips - 1):
-            outgoing(p, k).wait_recv()
+        wait_local(inbox.at[p, pl.ds(0, chips - 1)], out_recv.at[p])
         for k in range(chips - 1):
             total = total + inbox[p, k].astype(F32)
         out[:, p * BS : (p + 1) * BS] = total
@@ -414,8 +417,7 @@
     for p in range(2):
         swap(p).wait_send()
         pair(p).wait_send()
-        for k in range(chips - 1):
-            outgoing(p, k).wait_send()
+        wait_local(inbox.at[p, pl.ds(0, chips - 1)], out_send.at[p])
 
 
 def local(pressure_field, block_main, block_coupled, coupling, frequencies, receivers, floors):
@@ -428,12 +430,11 @@
     span = NT // (2 * chips)
     any_space = pl.BlockSpec(memory_space=pl.ANY)
     vmem = pl.BlockSpec(memory_space=pltpu.VMEM)
-    smem = pl.BlockSpec(memory_space=pltpu.SMEM)
     dma = pltpu.SemaphoreType.DMA
     summed = pl.pallas_call(
         functools.partial(kernel, nb, chips, 1.0 / math.sqrt(total_freq)),
         out_shape=jax.ShapeDtypeStruct((span, half), F32),
-        in_specs=[any_space] * 6 + [smem],
+        in_specs=[any_space] * 7,
         out_specs=vmem,
         scratch_shapes=[
             pltpu.VMEM((rows_here, width), BF16),
@@ -463,18 +464,19 @@
             pltpu.VMEM((1, width), F32),
             pltpu.VMEM((total_freq // BS, BS), F32),
             pltpu.VMEM((count // BS, BS), jnp.int32),
-            dma((nb,)),
-            dma((nb,)),
-            dma((nb,)),
+            pltpu.SMEM((STEPS,), jnp.int32),
+            dma,
             dma((3,)),
+            dma((3,)),
+            dma((4,)),
             dma((STEPS,)),
             dma((STEPS,)),
             dma((2,)),
             dma((2,)),
             dma((2,)),
             dma((2,)),
-            dma((2, chips)),
-            dma((2, chips)),
+            dma((2,)),
+            dma((2,)),
         ],
         compiler_params=pltpu.CompilerParams(
             collective_id=0, has_side_effects=True, vmem_limit_bytes=60 * 1024 * 1024

time: 48.9 us -> 45.8 us (0.937)
  Pallas kernels: 47.4 us -> 44.3 us
    pallas_call x1, Pallas kernels: 47.4 us -> 44.3 us  [local(): pl.pallas_call(functools.partial(kernel, nb, chips, 1.0 / math.sqrt(total...]
where the time goes in v5:
time: 45.8 us; the launch traced here: 45.7 us
  Pallas kernels  44.3 us (97%)
  local copies, waits for them, and re-layouts  1.38 us (3%)
    pallas_call x1, Pallas kernels, local(): pl.pallas_call(functools.partial(kernel, nb, chips, 1.0 / math.sqrt(total...  44.3 us
    unnamed x1, local copies, waits for them, and re-layouts  1.38 us

profile of v5, /device:TPU:1, one launch (start us, length us, event | category | flops | bytes accessed | tf_op | source)
XLA Modules:
  0.0 45.7 jit_solution(10757898087960038796)
XLA Ops:
  0.0 44.3 %march.1 = f32[32,256]{1,0:T(8,128)} custom-call(bf16[4096,256]{1,0:T(8,128)(2,1)} %field_hbm.1, bf16[24576,128]{1,0:T(8,128)(2,1)} %bitcast.6, bf16[24576,128]{1,0:T(8,128)(2,1)} %bitcast.7, f32[1,256]{1,0:T(1,128)} %bitcast.11, f32[64,128]{1,0:T(8,128)} %bitcast.9, s32[4,128]{1,0:T(4,128)} %bitcast.10, s32[4]{0:T(128)} %floors_hbm.1), custom_call_target="tpu_custom_call" | custom-call | tf_op jit(solution)/shard_map/march/pallas_call | solution.py:434
  44.3 1.4 %copy.9 = f32[256,32]{0,1:T(8,128)} copy(f32[256,32]{0,1:T(8,128)} %bitcast.8) | data formatting | bytes 65536

commit v6 on v5

--- a/solution.py
+++ b/solution.py
@@ -58,27 +58,15 @@
     return horner(COS_COEFFS, z), r * horner(SIN_COEFFS, z)
 
 
-def torus_offsets(chips):
+def send_order(chips):
     if chips != 32:
-        return None
-    found = []
-    for dx in range(4):
-        for dy in range(4):
-            for dh in range(2):
-                if dx or dy or dh:
-                    found.append((min(dx, 4 - dx) + min(dy, 4 - dy) + 2 * dh, dx, dy, dh))
-    return [entry[1:] for entry in sorted(found, key=lambda entry: (-entry[0],) + entry[1:])]
-
-
-def peers_of(chip, chips, sign):
-    offsets = torus_offsets(chips)
-    if offsets is None:
-        return [(chip + sign * k + chips) % chips for k in range(1, chips)]
-    x, y, h = chip // 8, (chip // 2) % 4, chip % 2
-    return [
-        (((x + sign * dx + 4) % 4) * 4 + (y + sign * dy + 4) % 4) * 2 + (h + dh) % 2
-        for dx, dy, dh in offsets
-    ]
+        return list(range(chips))
+
+    def reached(chip):
+        x, y, h = chip // 8, (chip // 2) % 4, chip % 2
+        return 1.25 * (x > 0) + 1.5 * (y > 0) + 2.0 * h + 0.01 * chip
+
+    return sorted(range(chips), key=reached)
 
 
 def kernel(
@@ -305,9 +293,9 @@
         return remote(source, target, halo_send.at[step], halo_recv.at[step], {"depth": other})
 
     wait_local(raw_field, field_sem)
-    load_group(0)
     for i in range(nb):
         put_raw(i + 1, raw_field[rows_of(i, BS), :])
+    load_group(0)
     for i in range(bounds[1]):
         bring_in(i)
         select(i)
@@ -383,41 +371,41 @@
         own[p, BS:, :] = mine[p][1] + arrived[p, BS:, :]
         pair(p).start()
 
-    targets = peers_of(chip, chips, 1)
-
-    def outgoing(p, k):
-        return remote(
-            sums.at[p, targets[k]],
-            inbox.at[p, k],
-            out_send.at[p],
-            out_recv.at[p],
-            {"freq": 2 * targets[k] + core},
-        )
-
+    rhs = []
     for p in range(2):
         pair(p).wait_recv()
-        rhs = jnp.concatenate([own[p, :BS, :], own[p, BS:, :], mate[p, :BS, :], mate[p, BS:, :]], axis=1)
-        group = min(8, chips)
-        for g in range(chips // group):
-            place = slice(g * group * span, (g + 1) * group * span)
-            lhs = jnp.concatenate([basis[q, place, :] for q in range(4)], axis=1)
-            part = (dot_nt(lhs, rhs) * factor).astype(BF16)
-            for u in range(group):
-                sums[p, g * group + u] = part[u * span : (u + 1) * span, :]
-        for k in range(chips - 1):
-            outgoing(p, k).start()
-
-    for p in range(2):
-        total = sums[p, chip].astype(F32)
-        wait_local(inbox.at[p, pl.ds(0, chips - 1)], out_recv.at[p])
-        for k in range(chips - 1):
-            total = total + inbox[p, k].astype(F32)
+        parts = (own[p, :BS, :], own[p, BS:, :], mate[p, :BS, :], mate[p, BS:, :])
+        rhs.append(jnp.concatenate(parts, axis=1))
+    rhs = jnp.concatenate(rhs, axis=0)
+    batch = min(8, chips)
+    for g in range(chips // batch):
+        place = slice(g * batch * span, (g + 1) * batch * span)
+        lhs = jnp.concatenate([basis[q, place, :] for q in range(4)], axis=1)
+        part = (dot_nt(lhs, rhs) * factor).astype(BF16)
+        for u in range(batch):
+            for p in range(2):
+                sums[g * batch + u, p] = part[u * span : (u + 1) * span, p * BS : (p + 1) * BS]
+    for target in send_order(chips):
+
+        @pl.when(target != chip)
+        def _():
+            remote(
+                sums.at[target], inbox.at[chip], out_send, out_recv, {"freq": 2 * target + core}
+            ).start()
+
+    inbox[chip] = sums[chip]
+    received = inbox.at[pl.ds(0, chips - 1)]
+    wait_local(received, out_recv)
+    for p in range(2):
+        total = inbox[0, p].astype(F32)
+        for j in range(1, chips):
+            total = total + inbox[j, p].astype(F32)
         out[:, p * BS : (p + 1) * BS] = total
 
+    wait_local(received, out_send)
     for p in range(2):
         swap(p).wait_send()
         pair(p).wait_send()
-        wait_local(inbox.at[p, pl.ds(0, chips - 1)], out_send.at[p])
 
 
 def local(pressure_field, block_main, block_coupled, coupling, frequencies, receivers, floors):
@@ -459,8 +447,8 @@
             pltpu.VMEM((4, NT // 2, BS), BF16),
             pltpu.VMEM((2, span, width), F32),
             pltpu.VMEM((2, chips, width), F32),
-            pltpu.VMEM((2, chips, span, BS), BF16),
-            pltpu.VMEM((2, chips, span, BS), BF16),
+            pltpu.VMEM((chips, 2, span, BS), BF16),
+            pltpu.VMEM((chips, 2, span, BS), BF16),
             pltpu.VMEM((1, width), F32),
             pltpu.VMEM((total_freq // BS, BS), F32),
             pltpu.VMEM((count // BS, BS), jnp.int32),
@@ -475,8 +463,8 @@
             dma((2,)),
             dma((2,)),
             dma((2,)),
-            dma((2,)),
-            dma((2,)),
+            dma,
+            dma,
         ],
         compiler_params=pltpu.CompilerParams(
             collective_id=0, has_side_effects=True, vmem_limit_bytes=60 * 1024 * 1024

time: 45.8 us -> 44.5 us (0.972)
  Pallas kernels: 44.3 us -> 42.9 us
    pallas_call x1, Pallas kernels: 44.3 us -> 42.9 us  [local(): pl.pallas_call(functools.partial(kernel, nb, chips, 1.0 / math.sqrt(total...]
where the time goes in v6:
time: 44.5 us; the launch traced here: 44.3 us
  Pallas kernels  42.9 us (96%)
  local copies, waits for them, and re-layouts  1.38 us (3%)
    pallas_call x1, Pallas kernels, local(): pl.pallas_call(functools.partial(kernel, nb, chips, 1.0 / math.sqrt(total...  42.9 us
    unnamed x1, local copies, waits for them, and re-layouts  1.38 us

profile of v6, /device:TPU:1, one launch (start us, length us, event | category | flops | bytes accessed | tf_op | source)
XLA Modules:
  0.0 44.3 jit_solution(8129128571593084809)
XLA Ops:
  0.0 42.9 %march.1 = f32[32,256]{1,0:T(8,128)} custom-call(bf16[4096,256]{1,0:T(8,128)(2,1)} %field_hbm.1, bf16[24576,128]{1,0:T(8,128)(2,1)} %bitcast.6, bf16[24576,128]{1,0:T(8,128)(2,1)} %bitcast.7, f32[1,256]{1,0:T(1,128)} %bitcast.11, f32[64,128]{1,0:T(8,128)} %bitcast.9, s32[4,128]{1,0:T(4,128)} %bitcast.10, s32[4]{0:T(128)} %floors_hbm.1), custom_call_target="tpu_custom_call" | custom-call | tf_op jit(solution)/shard_map/march/pallas_call | solution.py:422
  42.9 1.4 %copy.9 = f32[256,32]{0,1:T(8,128)} copy(f32[256,32]{0,1:T(8,128)} %bitcast.8) | data formatting | bytes 65536

commit v7 on v6

--- a/solution.py
+++ b/solution.py
@@ -327,8 +327,8 @@
     for step in range(1, STEPS):
         now, later = states[step % 2], states[1 - step % 2]
         turn = nb - 1 if step == STEPS - 1 else nb - 1 - between - (2 - step) * between
-        for i in list(range(turn)) + [nb - 1] + list(range(turn, nb - 1)):
-            if i == nb - 1:
+        for i in list(range(turn)) + [turn, nb - 1][turn // (nb - 1) :] + list(range(turn + 1, nb - 1)):
+            if i == turn:
                 arrival(step).wait()
                 put(now, nb + 1, halo[step, :BS, :], halo[step, BS:, :])
             real, imag = advance(step, now, i)

time: 44.5 us -> 44.5 us (level)
  no operation moved by 1% of the time
where the time goes in v7:
time: 44.5 us; the launch traced here: 44.2 us
  Pallas kernels  42.9 us (96%)
  local copies, waits for them, and re-layouts  1.38 us (3%)
    pallas_call x1, Pallas kernels, local(): pl.pallas_call(functools.partial(kernel, nb, chips, 1.0 / math.sqrt(total...  42.9 us
    unnamed x1, local copies, waits for them, and re-layouts  1.38 us

profile of v7, /device:TPU:1, one launch (start us, length us, event | category | flops | bytes accessed | tf_op | source)
XLA Modules:
  0.0 44.2 jit_solution(5939400311686331158)
XLA Ops:
  0.0 42.9 %march.1 = f32[32,256]{1,0:T(8,128)} custom-call(bf16[4096,256]{1,0:T(8,128)(2,1)} %field_hbm.1, bf16[24576,128]{1,0:T(8,128)(2,1)} %bitcast.6, bf16[24576,128]{1,0:T(8,128)(2,1)} %bitcast.7, f32[1,256]{1,0:T(1,128)} %bitcast.11, f32[64,128]{1,0:T(8,128)} %bitcast.9, s32[4,128]{1,0:T(4,128)} %bitcast.10, s32[4]{0:T(128)} %floors_hbm.1), custom_call_target="tpu_custom_call" | custom-call | tf_op jit(solution)/shard_map/march/pallas_call | solution.py:422
  42.9 1.4 %copy.9 = f32[256,32]{0,1:T(8,128)} copy(f32[256,32]{0,1:T(8,128)} %bitcast.8) | data formatting | bytes 65536
